TPU v7x, 32 devices: a whole 2x2x4 slice. The times are simulated.
32 devices in a mesh: gx: 4 (over y, core), gy: 8 (over z, x).
Axes of the slice: x: 2, y: 2, z: 4, core: 2. Of those that a mesh axis runs over, the one named last changes fastest.
Arguments:
- forcing: float32 [16, 256, 1024], P(None, 'gy', 'gx'), may hold values from -6 to 6
- damping: float32 [16, 256, 1024], P(None, 'gy', 'gx'), may hold values from 0.5 to 4
- coupling: float32 [16, 16], replicated, may hold values from -1.5 to 1.5
- wind_lon: float32 [256, 1024], P('gy', 'gx'), may hold values from -0.5 to 0.5
- wind_lat: float32 [256, 1024], P('gy', 'gx'), may hold values from -0.5 to 0.5
Outputs:
- solution: float32 [16, 256, 1024], P(None, 'gy', 'gx')
- residual: float32 [16, 256, 1024], P(None, 'gy', 'gx')
All inputs are finite; a program needn't handle non-finite values.
Results may differ from a plain program's by a relative error of at most 0.0003.
Values sent between devices are 32-bit elements; how exact they have to be, the bound alone decides.
A program may use at most 64 MiB of HBM per device.

v0:
```python
import functools
import math

import jax
import jax.numpy as jnp
from jax import lax
from jax.experimental import pallas as pl
from jax.experimental.pallas import tpu as pltpu
from jax.sharding import PartitionSpec as P

ITERS = 8
COUPLE = 0.25
DIFF_LAT = 0.5
DIFF_LON = 0.5
GUARD = 1.0
MESH = pl.DeviceIdType.MESH
HI = lax.Precision.HIGHEST

MIDDLE = 9.0
RADIUS = 6.0
WIDTH = 3.0
THETA = [MIDDLE + RADIUS * math.cos(math.pi * (2 * k + 1) / (2 * ITERS)) for k in (7, 0, 4, 2, 6, 1, 5, 3)]
PAIRS = [(k, i) for k in range(ITERS + 1) for i in range(k + 1)]
GROUP = 4
HALO = 4
BLOCKS = ITERS // 2


def apply_to(coords):
    out = [None] * (len(coords) + 1)
    for k, value in enumerate(coords):
        low = THETA[k] * value if k < ITERS else value
        out[k] = low if out[k] is None else out[k] + low
        out[k + 1] = WIDTH * value
    return out


def small_solve(gram):
    first = jnp.sqrt(gram[0][0] + GUARD)
    coords = [[1.0 / first]]
    images = [[gram[i][0] * coords[0][0] for i in range(ITERS + 1)]]
    heights = []
    for j in range(ITERS):
        moved = apply_to(coords[j])
        column = []
        for i in range(j + 1):
            column.append(functools.reduce(lambda a, b: a + b, [images[i][k] * moved[k] for k in range(j + 2)]))
        left = list(moved)
        for i in range(j + 1):
            for k in range(i + 1):
                left[k] = left[k] - column[i] * coords[i][k]
        image = [
            functools.reduce(lambda a, b: a + b, [gram[r][k] * left[k] for k in range(j + 2)])
            for r in range(ITERS + 1)
        ]
        norm_sq = functools.reduce(lambda a, b: a + b, [image[k] * left[k] for k in range(j + 2)])
        subdiag = jnp.sqrt(jnp.maximum(norm_sq, 0.0) + GUARD)
        column.append(subdiag)
        heights.append(column)
        inverse = 1.0 / subdiag
        coords.append([v * inverse for v in left])
        images.append([v * inverse for v in image])
    cosines, sines, target, rotated = [], [], [first], []
    for j in range(ITERS):
        column = list(heights[j])
        for e in range(j):
            upper, lower = column[e], column[e + 1]
            column[e] = cosines[e] * upper + sines[e] * lower
            column[e + 1] = cosines[e] * lower - sines[e] * upper
        upper, lower = column[j], column[j + 1]
        radius = jnp.sqrt(upper * upper + lower * lower)
        inverse = 1.0 / radius
        cosine, sine = upper * inverse, lower * inverse
        column[j] = radius
        kept = target[j]
        target[j] = cosine * kept
        target.append(-sine * kept)
        cosines.append(cosine)
        sines.append(sine)
        rotated.append(column)
    weights = [None] * ITERS
    for j in reversed(range(ITERS)):
        value = target[j]
        for later in range(j + 1, ITERS):
            value = value - rotated[later][j] * weights[later]
        weights[j] = value / rotated[j][j]
    answer = [None] * ITERS
    for j in range(ITERS):
        for k in range(j + 1):
            term = weights[j] * coords[j][k]
            answer[k] = term if answer[k] is None else answer[k] + term
    return answer, apply_to(answer)


def kernel(nx, ny, f_hbm, d_hbm, c_ref, wl_hbm, wa_hbm, basis, splats,
           diag, coef, block, single, side_in, side_out, band, fixed_in, fixed_out, corner_in, corner_out,
           gram_acc, mine, slots, wl_ref, wa_ref,
           in_sem, wind_sem, lat_send, lat_recv, lon_send, lon_recv, turn_send, turn_recv, fix_send, fix_recv, red_send, red_recv):
    channels, lat, lon = f_hbm.shape
    tiles = lon // 128
    total = nx * ny
    ix, iy = lax.axis_index("gx"), lax.axis_index("gy")
    me = ix * ny + iy
    east, west = lax.rem(ix + 1, nx), lax.rem(ix + nx - 1, nx)

    winds = [pltpu.make_async_copy(wl_hbm, wl_ref, wind_sem.at[0]), pltpu.make_async_copy(wa_hbm, wa_ref, wind_sem.at[1])]
    for copy in winds:
        copy.start()
    loads = []
    for q, (src, dst, off) in enumerate(((f_hbm, basis.at[0], HALO), (d_hbm, diag, 2))):
        for c in range(channels):
            copy = pltpu.make_async_copy(src.at[c], dst.at[pl.ds(off, lat), c, :], in_sem.at[q, c])
            copy.start()
            loads.append(copy)

    barrier = pltpu.get_barrier_semaphore()

    def greet(o, _):
        other = lax.rem(me + o, total)
        pl.semaphore_signal(barrier, inc=1, device_id=(other // ny, lax.rem(other, ny)), device_id_type=MESH)
        return 0

    lax.fori_loop(1, total, greet, 0)

    scale = 1.0 / WIDTH
    size = GROUP * channels

    def spread(n):
        row = lax.broadcasted_iota(jnp.int32, (n, channels), 0)
        col = lax.broadcasted_iota(jnp.int32, (n, channels), 1)
        return jnp.where(lax.rem(row, channels) == col, 1.0, 0.0).astype(jnp.float32)

    def widen(tall, n):
        wide = lax.dot_general(tall, spread(3 * n), (((1,), (1,)), ((), ())), precision=HI,
                               preferred_element_type=jnp.float32) * (COUPLE * scale)
        across = lax.broadcasted_iota(jnp.int32, wide.shape, 1)
        high = wide.astype(jnp.bfloat16).astype(jnp.float32)
        return jnp.where(across < 2 * n, high, wide - high), across

    single[...] = widen(c_ref[...], channels)[0].astype(jnp.bfloat16)
    tall = lax.dot_general(spread(size), c_ref[...], (((1,), (0,)), ((), ())), precision=HI,
                           preferred_element_type=jnp.float32)
    wide, across = widen(tall, size)
    down = lax.broadcasted_iota(jnp.int32, (size, 3 * size), 0)
    block[...] = jnp.where(down // channels == lax.rem(across, size) // channels, wide, 0.0).astype(jnp.bfloat16)

    def blank(at):
        for b in range(BLOCKS):
            basis[2 * b, pl.ds(HALO + lat if at else 0, HALO)] = jnp.zeros((HALO, channels, lon), jnp.float32)
        diag[pl.ds(lat + 2 if at else 0, 2)] = jnp.zeros((2, channels, lon), jnp.float32)
        coef[pl.ds(lat + 2 if at else 0, 2)] = jnp.zeros((2, 8, lon), jnp.float32)
        corner_in[:, 0 if at else 2] = jnp.zeros((BLOCKS, 2, 128), jnp.float32)
        corner_in[:, 1 if at else 3] = jnp.zeros((BLOCKS, 2, 128), jnp.float32)

    @pl.when(iy == 0)
    def _():
        blank(0)

    @pl.when(iy == ny - 1)
    def _():
        blank(1)

    for copy in winds:
        copy.wait()
    place = (lax.broadcasted_iota(jnp.int32, (lat, 128), 0) + iy * lat).astype(jnp.float32)
    phi = -math.pi / 2 + (place + 0.5) * (math.pi / (lat * ny))
    kx = (DIFF_LON * scale) / (jnp.cos(phi) ** 2 + 0.1)
    wl = wl_ref[...] * (scale / 12.0)
    wa = wa_ref[...] * (scale / 12.0)
    kx = jnp.concatenate([kx] * tiles, axis=1)
    planes = (8.0 * wl - kx, -8.0 * wl - kx, wl, 8.0 * wa - DIFF_LAT * scale, -8.0 * wa - DIFF_LAT * scale, wa,
              2.0 * kx + (1.0 + 2.0 * DIFF_LAT) * scale)
    for q, plane in enumerate(planes + (jnp.zeros_like(kx),)):
        for r in range(lat):
            coef[r + 2, q:q + 1, :] = plane[r:r + 1, :]

    for copy in loads:
        copy.wait()

    def prepare(r, _):
        diag[r + 2] = diag[r + 2] * scale + coef[r + 2, 6:7, :]
        return 0

    lax.fori_loop(0, lat, prepare, 0)

    def pack(read, far, n):
        lane = lax.broadcasted_iota(jnp.int32, (n, 128), 1)
        to_west = to_east = jnp.zeros((n, 128), jnp.float32)
        for r in range(lat):
            head = read(r, slice(0, 128))
            tail = read(r, slice(lon - 128, lon))
            here = (lane >= 2 * r) & (lane < 2 * r + 2)
            to_west = jnp.where(here, pltpu.roll(head, 2 * r, 1) if r else head, to_west)
            to_east = jnp.where(here, pltpu.roll(tail, (2 * r + 2) % 128, 1), to_east)
            if far:
                here = (lane >= 64 + 2 * r) & (lane < 64 + 2 * r + 2)
                to_west = jnp.where(here, pltpu.roll(head, (62 + 2 * r) % 128, 1), to_west)
                to_east = jnp.where(here, pltpu.roll(tail, (68 + 2 * r) % 128, 1), to_east)
        return to_west, to_east

    fixed = [pack(lambda r, cut: diag[r + 2, :, cut], False, channels), pack(lambda r, cut: coef[r + 2, :, cut], False, 8)]
    for way in range(2):
        fixed_out[way, 0:channels, :] = fixed[0][way]
        fixed_out[way, channels:channels + 8, :] = fixed[1][way]

    lane = lax.broadcasted_iota(jnp.int32, (channels, 128), 1)
    spot = lax.broadcasted_iota(jnp.int32, (8, 128), 1)
    deep = lax.broadcasted_iota(jnp.int32, (8, 128), 0)

    def copy_to(src, dst, send, recv, to):
        return pltpu.make_async_remote_copy(src_ref=src, dst_ref=dst, send_sem=send, recv_sem=recv,
                                            device_id=to, device_id_type=MESH)

    def lat_to(way):
        return iy + 1 if way else iy - 1

    def lat_copy(b, way):
        src = pl.ds(lat, HALO) if way else pl.ds(HALO, HALO)
        dst = pl.ds(0, HALO) if way else pl.ds(lat + HALO, HALO)
        return copy_to(basis.at[2 * b, src], basis.at[2 * b, dst], lat_send.at[b, way], lat_recv.at[b, way], (ix, lat_to(way)))

    def fix_copies(way):
        src = pl.ds(lat, 2) if way else pl.ds(2, 2)
        dst = pl.ds(0, 2) if way else pl.ds(lat + 2, 2)
        return [copy_to(ref.at[src], ref.at[dst], fix_send.at[n, way], fix_recv.at[n, way], (ix, lat_to(way)))
                for n, ref in enumerate((diag, coef))]

    def fix_side(way):
        return copy_to(fixed_out.at[way], fixed_in.at[way], fix_send.at[2, way], fix_recv.at[2, way],
                       (east if way else west, iy))

    def lon_copy(b, way):
        return copy_to(side_out.at[b, way], side_in.at[b, way], lon_send.at[b, way], lon_recv.at[b, way],
                       (east if way else west, iy))

    def turn_copy(b, up, way):
        n = 2 * up + way
        return copy_to(corner_out.at[b], corner_in.at[b, n], turn_send.at[b, n], turn_recv.at[b, n],
                       (east if way else west, lat_to(up)))

    def each_lat(act):
        @pl.when(iy < ny - 1)
        def _():
            act(1)

        @pl.when(iy > 0)
        def _():
            act(0)

    def arrive_lat(act):
        @pl.when(iy > 0)
        def _():
            act(1)

        @pl.when(iy < ny - 1)
        def _():
            act(0)

    def send_side(b):
        k = 2 * b
        to_west, to_east = pack(lambda r, cut: basis[k, r + HALO, :, cut], True, channels)
        side_out[b, 0] = to_west
        side_out[b, 1] = to_east
        lon_copy(b, 0).start()
        lon_copy(b, 1).start()
        small = jnp.zeros((8, 128), jnp.float32)
        for up in range(2):
            for way, ref in enumerate((to_west, to_east)):
                for h in range(channels // 8):
                    at = 16 * up + 8 * way + 4 * h
                    here = (spot >= at) & (spot < at + 4)
                    start = 2 * lat - 4 if up else 0
                    part = ref[8 * h:8 * h + 8, :]
                    small = jnp.where(here, pltpu.roll(part, (at - start) % 128, 1) if at != start else part, small)
        dense = small
        for g in range(1, 4):
            moved = pltpu.roll(pltpu.roll(small, 8 - 2 * g, 0), 32 * g, 1)
            dense = jnp.where(spot // 32 == g, moved, dense)
        corner_out[b] = dense[0:2, :]

        def go(up):
            turn_copy(b, up, 0).start()
            turn_copy(b, up, 1).start()

        each_lat(go)

    def take_corners(b):
        got = jnp.zeros((2, 128), jnp.float32)
        sub = lax.rem(lax.broadcasted_iota(jnp.int32, (2, 128), 1), 32) // 8
        for n in range(4):
            got = jnp.where(sub == n, corner_in[b, n], got)
        got = jnp.concatenate([got] * 4, axis=0)
        small = got
        for g in range(1, 4):
            small = jnp.where(deep // 2 == g, pltpu.roll(got, 128 - 32 * g, 1), small)
        parts = []
        for h in range(channels // 8):
            part = jnp.zeros((8, 128), jnp.float32)
            for up in range(2):
                for way in range(2):
                    at = 16 * up + 8 * way + 4 * h
                    want = (64 if way else 0) + (2 * lat - 4 if up else 0)
                    here = (spot >= want) & (spot < want + 4)
                    part = jnp.where(here, pltpu.roll(small, (want - at) % 128, 1) if want != at else small, part)
            parts.append(part)
        return jnp.concatenate(parts, axis=0)

    def theta_of(k):
        theta = jnp.float32(THETA[0] * scale)
        for i in range(1, ITERS):
            theta = jnp.where(k == i, jnp.float32(THETA[i] * scale), theta)
        return theta

    def dots(k, first, count):
        def one(i, _):
            def part(b, acc):
                acc = list(acc)
                for j in range(8):
                    r = b * 8 + j + HALO + first
                    prod = basis[k, r] * basis[i, r]
                    n = 0
                    for h in range(channels // 8):
                        for t in range(tiles):
                            acc[n % 4] = acc[n % 4] + prod[8 * h:8 * h + 8, 128 * t:128 * t + 128]
                            n += 1
                return tuple(acc)

            zero = jnp.zeros((8, 128), jnp.float32)
            acc = lax.fori_loop(0, count // 8, part, (zero,) * 4)
            gram_acc[lax.div(k * (k + 1), 2) + i] = (acc[0] + acc[1]) + (acc[2] + acc[3])
            return 0

        lax.fori_loop(0, k + 1, one, 0)

    def split(stack):
        high = stack.astype(jnp.bfloat16)
        low = (stack - high.astype(jnp.float32)).astype(jnp.bfloat16)
        return jnp.concatenate([high, low, high], axis=0)

    def rows(k, picked, theta, beside, bare=False):
        stack = jnp.concatenate([basis[k, r + HALO] for r in picked], axis=0)
        mixed = lax.dot_general(block[...], split(stack), (((1,), (0,)), ((), ())), preferred_element_type=jnp.float32)
        for j, r in enumerate(picked):
            inside = 0 <= r < lat
            source = beside[0] if inside else beside[1]
            left = 2 * r if inside else 64 + 2 * (r % lat)
            right = 64 + 2 * r if inside else 2 * (r % lat)

            def turn(v, shift):
                return pltpu.roll(v, shift % 128, 1) if shift % 128 else v

            x = [basis[k, r + HALO, :, 128 * t:128 * t + 128] for t in range(tiles)]
            fwd1 = [pltpu.roll(v, 127, 1) for v in x] + [turn(source, 127 - right)]
            fwd2 = [pltpu.roll(v, 126, 1) for v in x] + [turn(source, 126 - right)]
            bwd1 = [turn(source, -left - 1)] + [pltpu.roll(v, 1, 1) for v in x]
            bwd2 = [turn(source, -left)] + [pltpu.roll(v, 2, 1) for v in x]
            for t in range(tiles):
                cut = slice(128 * t, 128 * t + 128)
                e1 = jnp.where(lane < 127, fwd1[t], fwd1[t + 1])
                e2 = jnp.where(lane < 126, fwd2[t], fwd2[t + 1])
                w1 = jnp.where(lane >= 1, bwd1[t + 1], bwd1[t])
                w2 = jnp.where(lane >= 2, bwd2[t + 1], bwd2[t])

                def weight(q):
                    return coef[r + 2, q:q + 1, cut]

                def near(d):
                    return basis[k, r + HALO + d, :, cut]

                def has(d):
                    return not bare or 0 <= r + d < lat

                value = (diag[r + 2, :, cut] - theta) * x[t] + mixed[channels * j:channels * (j + 1), cut]
                value = value + (weight(0) * e1 + weight(1) * w1 + weight(2) * (w2 - e2))
                if has(1):
                    value = value + weight(3) * near(1)
                if has(-1):
                    value = value + weight(4) * near(-1)
                if has(2) and has(-2):
                    value = value + weight(5) * (near(-2) - near(2))
                elif has(2):
                    value = value - weight(5) * near(2)
                else:
                    value = value + weight(5) * near(-2)
                basis[k + 1, r + HALO, :, cut] = value

    def middle(b):
        from_east, from_west = side_in[b, 0], side_in[b, 1]
        return jnp.where(lane < 64, from_west, pltpu.roll(from_east, 64, 1))

    def edge_band(b, theta, centre, corners):
        from_east, from_west = side_in[b, 0], side_in[b, 1]
        to_west, to_east = side_out[b, 0], side_out[b, 1]
        low = jnp.where(lane < 64, pltpu.roll(from_west, 64, 1), pltpu.roll(to_east, 64, 1))
        high = jnp.where(lane < 64, to_west, from_east)
        even = lax.rem(lane, 2) == 0
        e1 = jnp.where(even, pltpu.roll(centre, 127, 1), pltpu.roll(high, 1, 1))
        w1 = jnp.where(even, pltpu.roll(low, 127, 1), pltpu.roll(centre, 1, 1))
        row = lax.rem(lane, 64) // 2
        n1 = jnp.where(row < lat - 1, pltpu.roll(centre, 126, 1), pltpu.roll(corners, 126, 1))
        n2 = jnp.where(row < lat - 2, pltpu.roll(centre, 124, 1), pltpu.roll(corners, 124, 1))
        s1 = jnp.where(row >= 1, pltpu.roll(centre, 2, 1), pltpu.roll(corners, 2, 1))
        s2 = jnp.where(row >= 2, pltpu.roll(centre, 4, 1), pltpu.roll(corners, 4, 1))
        mixed = lax.dot_general(single[...], split(centre), (((1,), (0,)), ((), ())), preferred_element_type=jnp.float32)
        own = jnp.where(lane < 64, fixed_in[1, 0:channels, :], pltpu.roll(fixed_in[0, 0:channels, :], 64, 1))
        tail = jnp.where(spot < 64, fixed_in[1, channels:channels + 8, :],
                         pltpu.roll(fixed_in[0, channels:channels + 8, :], 64, 1))

        def weight(q):
            return tail[q:q + 1, :]

        value = (own - theta) * centre + mixed
        value = value + (weight(0) * e1 + weight(1) * w1 + weight(2) * (low - high))
        value = value + weight(3) * n1 + weight(4) * s1 + weight(5) * (s2 - n2)
        band[...] = value

    def stage(b, _):
        k = 2 * b
        theta, after = theta_of(k), theta_of(k + 1)

        @pl.when(b > 0)
        def _():
            dots(k - 1, 0, lat)

        dots(k, 0, lat)
        lon_copy(b, 0).wait()
        lon_copy(b, 1).wait()
        centre = middle(b)
        for g in range((lat - 4) // GROUP):
            rows(k, [2 + GROUP * g + j for j in range(GROUP)], theta, (centre, None))
        rows(k, (0, 1, lat - 2, lat - 1), theta, (centre, None), bare=True)

        @pl.when(b == 0)
        def _():
            fix_side(0).wait()
            fix_side(1).wait()

        def corners_in(up):
            turn_copy(b, up, 0).wait_recv()
            turn_copy(b, up, 1).wait_recv()

        arrive_lat(corners_in)
        corners = take_corners(b)
        edge_band(b, theta, centre, corners)
        beside = band[...]
        for g in range((lat - 8) // GROUP):
            rows(k + 1, [4 + GROUP * g + j for j in range(GROUP)], after, (beside, None))

        def halo_in(way):
            lat_copy(b, way).wait_recv()

            @pl.when(b == 0)
            def _():
                for copy in fix_copies(way):
                    copy.wait_recv()

        arrive_lat(halo_in)
        rows(k, (-2, -1, lat, lat + 1), theta, (None, corners))
        south, north = basis[k, HALO - 1], basis[k, HALO + lat]
        basis[k + 1, HALO] += coef[2, 4:5, :] * south + coef[2, 5:6, :] * basis[k, HALO - 2]
        basis[k + 1, HALO + 1] += coef[3, 5:6, :] * south
        basis[k + 1, HALO + lat - 1] += coef[lat + 1, 3:4, :] * north - coef[lat + 1, 5:6, :] * basis[k, HALO + lat + 1]
        basis[k + 1, HALO + lat - 2] -= coef[lat, 5:6, :] * north
        rows(k + 1, tuple(range(4)), after, (beside, None))
        rows(k + 1, tuple(range(lat - 4, lat)), after, (beside, None))

        @pl.when(b + 1 < BLOCKS)
        def _():
            each_lat(lambda way: lat_copy(b + 1, way).start())
            send_side(b + 1)

        def sent(way):
            lat_copy(b, way).wait_send()
            turn_copy(b, way, 0).wait_send()
            turn_copy(b, way, 1).wait_send()

            @pl.when(b == 0)
            def _():
                for copy in fix_copies(way):
                    copy.wait_send()

        each_lat(sent)
        return 0

    pl.semaphore_wait(barrier, total - 1)
    each_lat(lambda way: lat_copy(0, way).start())
    send_side(0)
    fix_side(0).start()
    fix_side(1).start()

    def give_fixed(way):
        for copy in fix_copies(way):
            copy.start()

    each_lat(give_fixed)
    lax.fori_loop(0, BLOCKS, stage, 0)
    dots(ITERS - 1, 0, lat)
    dots(ITERS, 0, lat)

    sums = jnp.concatenate(
        [jnp.sum(gram_acc[n], axis=0, keepdims=True) for n in range(len(PAIRS))]
        + [jnp.zeros((128 - len(PAIRS), 128), jnp.float32)], axis=0)
    flat = lax.dot_general(jnp.ones((8, 128), jnp.float32), sums, (((1,), (1,)), ((), ())), precision=HI,
                           preferred_element_type=jnp.float32)
    mine[...] = flat[0:1, :]
    slots[me] = flat[0:1, :]

    def share(o):
        other = lax.rem(me + o, total)
        return pltpu.make_async_remote_copy(
            src_ref=mine, dst_ref=slots.at[me], send_sem=red_send.at[o], recv_sem=red_recv.at[me],
            device_id=(other // ny, lax.rem(other, ny)), device_id_type=MESH)

    def take(o):
        other = lax.rem(me + total - o, total)
        return pltpu.make_async_remote_copy(
            src_ref=mine, dst_ref=slots.at[other], send_sem=red_send.at[o], recv_sem=red_recv.at[other],
            device_id=(other // ny, lax.rem(other, ny)), device_id_type=MESH)

    def give(o, _):
        share(o).start()
        return 0

    def get(o, _):
        take(o).wait_recv()
        share(o).wait_send()
        return 0

    lax.fori_loop(1, total, give, 0)
    lax.fori_loop(1, total, get, 0)
    whole = slots[0]
    for n in range(1, total):
        whole = whole + slots[n]
    gram = [[None] * (ITERS + 1) for _ in range(ITERS + 1)]
    for n, (k, i) in enumerate(PAIRS):
        gram[k][i] = gram[i][k] = jnp.broadcast_to(whole[:, n:n + 1], (8, 128))
    answer, applied = small_solve(gram)
    for k in range(ITERS):
        splats[k] = answer[k]
    for k in range(ITERS + 1):
        splats[ITERS + k] = applied[k]


def finish(b_ref, w_ref, sol_hbm, res_hbm, outs, out_sem):
    channels, lat, lon = sol_hbm.shape
    stores = []
    for part in range(lat // 8):
        def one(j, _):
            r = 8 * part + j
            for h in range(channels // 8):
                for t in range(lon // 128):
                    at = (slice(8 * h, 8 * h + 8), slice(128 * t, 128 * t + 128))
                    x = b_ref[0, r + HALO, at[0], at[1]]
                    best = w_ref[0] * x
                    rest = x - w_ref[ITERS] * x
                    for k in range(1, ITERS + 1):
                        x = b_ref[k, r + HALO, at[0], at[1]]
                        if k < ITERS:
                            best = best + w_ref[k] * x
                        rest = rest - w_ref[ITERS + k] * x
                    outs[0, r, at[0], at[1]] = best
                    outs[1, r, at[0], at[1]] = rest
            return 0

        lax.fori_loop(0, 8, one, 0)
        for q, dst in enumerate((sol_hbm, res_hbm)):
            for c in range(channels):
                copy = pltpu.make_async_copy(outs.at[q, pl.ds(8 * part, 8), c, :], dst.at[c, pl.ds(8 * part, 8), :],
                                             out_sem.at[part, q, c])
                copy.start()
                stores.append(copy)
    for copy in stores:
        copy.wait()


def solution(mesh):
    nx, ny = mesh.shape["gx"], mesh.shape["gy"]

    def per_device(forcing, damping, coupling, wind_lon, wind_lat):
        channels, lat, lon = forcing.shape
        f32 = jnp.float32
        vmem = pl.BlockSpec(memory_space=pltpu.VMEM)
        hbm = pl.BlockSpec(memory_space=pltpu.HBM)
        dma = pltpu.SemaphoreType.DMA

        def keep(v):
            return pltpu.with_memory_space_constraint(v, pltpu.HBM)

        basis, weights = pl.pallas_call(
            functools.partial(kernel, nx, ny),
            out_shape=(pltpu.VMEM((ITERS + 1, lat + 2 * HALO, channels, lon), f32), pltpu.VMEM((2 * ITERS + 1, 8, 128), f32)),
            in_specs=[hbm, hbm, vmem, hbm, hbm],
            out_specs=(vmem, vmem),
            scratch_shapes=[
                pltpu.VMEM((lat + 4, channels, lon), f32),
                pltpu.VMEM((lat + 4, 8, lon), f32),
                pltpu.VMEM((GROUP * channels, 3 * GROUP * channels), jnp.bfloat16),
                pltpu.VMEM((channels, 3 * channels), jnp.bfloat16),
                pltpu.VMEM((BLOCKS, 2, channels, 128), f32),
                pltpu.VMEM((BLOCKS, 2, channels, 128), f32),
                pltpu.VMEM((channels, 128), f32),
                pltpu.VMEM((2, channels + 8, 128), f32),
                pltpu.VMEM((2, channels + 8, 128), f32),
                pltpu.VMEM((BLOCKS, 4, 2, 128), f32),
                pltpu.VMEM((BLOCKS, 2, 128), f32),
                pltpu.VMEM((len(PAIRS), 8, 128), f32),
                pltpu.VMEM((1, 128), f32),
                pltpu.VMEM((nx * ny, 1, 128), f32),
                pltpu.VMEM((lat, lon), f32), pltpu.VMEM((lat, lon), f32),
                dma((2, channels)), dma((2,)),
                dma((BLOCKS, 2)), dma((BLOCKS, 2)), dma((BLOCKS, 2)), dma((BLOCKS, 2)),
                dma((BLOCKS, 4)), dma((BLOCKS, 4)), dma((3, 2)), dma((3, 2)),
                dma((nx * ny,)), dma((nx * ny,)),
            ],
            compiler_params=pltpu.CompilerParams(
                collective_id=0, has_side_effects=True, vmem_limit_bytes=24 * 1024 * 1024),
        )(keep(forcing), keep(damping), coupling, keep(wind_lon), keep(wind_lat))
        shape = jax.ShapeDtypeStruct((channels, lat, lon), f32)
        return pl.pallas_call(
            finish,
            out_shape=(shape, shape),
            in_specs=[vmem, vmem],
            out_specs=(hbm, hbm),
            scratch_shapes=[pltpu.VMEM((2, lat, channels, lon), f32), dma((lat // 8, 2, channels))],
            compiler_params=pltpu.CompilerParams(vmem_limit_bytes=24 * 1024 * 1024),
        )(basis, weights)

    return jax.shard_map(
        per_device,
        mesh=mesh,
        in_specs=(P(None, "gy", "gx"), P(None, "gy", "gx"), P(), P("gy", "gx"), P("gy", "gx")),
        out_specs=(P(None, "gy", "gx"), P(None, "gy", "gx")),
        check_vma=False,
    )
```

profile of v0, /device:TPU:0, one launch (start us, length us, event | category | flops | bytes accessed | tf_op | source)
XLA Modules:
  0.0 45.2 jit_solution(13537701263836297196)
XLA Ops:
  0.6 0.0 copy-start
  0.6 0.7 %copy-done = f32[16,16]{1,0:T(8,128)S(1)} copy-done((f32[16,16]{1,0:T(8,128)S(1)}, f32[16,16]{1,0:T(8,128)}, u32[]{:S(2)}) %copy-start) | copy-done | bytes 1048
  1.3 40.7 %shard_map.68 = (f32[9,40,16,256]{3,2,1,0:T(8,128)S(1)}, f32[17,8,128]{2,1,0:T(8,128)S(1)}) custom-call(f32[16,32,256]{2,1,0:T(8,128)} %f_hbm.1, f32[16,32,256]{2,1,0:T(8,128)} %d_hbm.1, f32[16,16]{1,0:T(8,128)S(1)} %copy-done, f32[32,256]{1,0:T(8,128)} %wl_hbm.1, f32[32,256]{1,0:T(8,128)} %wa_hbm.1), custom_call_target="tpu_custom_call" | custom-call | tf_op jit(solution)/shard_map/pallas_call | solution.py:589
  42.1 3.1 %shard_map.69 = (f32[16,32,256]{2,1,0:T(8,128)}, f32[16,32,256]{2,1,0:T(8,128)}) custom-call(f32[9,40,16,256]{3,2,1,0:T(8,128)S(1)} %get-tuple-element.4.b_ref, f32[17,8,128]{2,1,0:T(8,128)S(1)} %get-tuple-element.5.w_ref), custom_call_target="tpu_custom_call" | custom-call | tf_op jit(solution)/shard_map/pallas_call | solution.py:619
Async XLA Ops:
  0.6 0.7 %copy-start = (f32[16,16]{1,0:T(8,128)S(1)}, f32[16,16]{1,0:T(8,128)}, u32[]{:S(2)}) copy-start(f32[16,16]{1,0:T(8,128)} %c_ref.1) | copy-start | bytes 3076
where the time goes:
time: 45.4 us; the launch traced here: 45.2 us
  Pallas kernels  43.9 us (97%)
  local copies, waits for them, and re-layouts  0.69 us (2%)
  between operations  0.65 us (1%)
    pallas_call x1, Pallas kernels, per_device(): pl.pallas_call(functools.partial(kernel, nx, ny), out_shape=(pltpu.VMEM((...  40.7 us
    pallas_call x1, Pallas kernels, per_device(): pl.pallas_call(finish, out_shape=(shape, shape), in_specs=[vmem, vmem], o...  3.11 us

commit v1 on v0

--- a/solution.py
+++ b/solution.py
@@ -92,9 +92,9 @@
     return answer, apply_to(answer)
 
 
-def kernel(nx, ny, f_hbm, d_hbm, c_ref, wl_hbm, wa_hbm, basis, splats,
+def kernel(nx, ny, f_hbm, d_hbm, c_hbm, wl_hbm, wa_hbm, basis, splats,
            diag, coef, block, single, side_in, side_out, band, fixed_in, fixed_out, corner_in, corner_out,
-           gram_acc, mine, slots, wl_ref, wa_ref,
+           gram_acc, mine, slots, c_ref, wl_ref, wa_ref,
            in_sem, wind_sem, lat_send, lat_recv, lon_send, lon_recv, turn_send, turn_recv, fix_send, fix_recv, red_send, red_recv):
     channels, lat, lon = f_hbm.shape
     tiles = lon // 128
@@ -103,15 +103,16 @@
     me = ix * ny + iy
     east, west = lax.rem(ix + 1, nx), lax.rem(ix + nx - 1, nx)
 
-    winds = [pltpu.make_async_copy(wl_hbm, wl_ref, wind_sem.at[0]), pltpu.make_async_copy(wa_hbm, wa_ref, wind_sem.at[1])]
-    for copy in winds:
-        copy.start()
-    loads = []
+    loads = [[], []]
     for q, (src, dst, off) in enumerate(((f_hbm, basis.at[0], HALO), (d_hbm, diag, 2))):
         for c in range(channels):
             copy = pltpu.make_async_copy(src.at[c], dst.at[pl.ds(off, lat), c, :], in_sem.at[q, c])
             copy.start()
-            loads.append(copy)
+            loads[q].append(copy)
+    small = [pltpu.make_async_copy(src, dst, wind_sem.at[n])
+             for n, (src, dst) in enumerate(((wl_hbm, wl_ref), (wa_hbm, wa_ref), (c_hbm, c_ref)))]
+    for copy in small:
+        copy.start()
 
     barrier = pltpu.get_barrier_semaphore()
 
@@ -136,13 +137,6 @@
         across = lax.broadcasted_iota(jnp.int32, wide.shape, 1)
         high = wide.astype(jnp.bfloat16).astype(jnp.float32)
         return jnp.where(across < 2 * n, high, wide - high), across
-
-    single[...] = widen(c_ref[...], channels)[0].astype(jnp.bfloat16)
-    tall = lax.dot_general(spread(size), c_ref[...], (((1,), (0,)), ((), ())), precision=HI,
-                           preferred_element_type=jnp.float32)
-    wide, across = widen(tall, size)
-    down = lax.broadcasted_iota(jnp.int32, (size, 3 * size), 0)
-    block[...] = jnp.where(down // channels == lax.rem(across, size) // channels, wide, 0.0).astype(jnp.bfloat16)
 
     def blank(at):
         for b in range(BLOCKS):
@@ -159,29 +153,6 @@
     @pl.when(iy == ny - 1)
     def _():
         blank(1)
-
-    for copy in winds:
-        copy.wait()
-    place = (lax.broadcasted_iota(jnp.int32, (lat, 128), 0) + iy * lat).astype(jnp.float32)
-    phi = -math.pi / 2 + (place + 0.5) * (math.pi / (lat * ny))
-    kx = (DIFF_LON * scale) / (jnp.cos(phi) ** 2 + 0.1)
-    wl = wl_ref[...] * (scale / 12.0)
-    wa = wa_ref[...] * (scale / 12.0)
-    kx = jnp.concatenate([kx] * tiles, axis=1)
-    planes = (8.0 * wl - kx, -8.0 * wl - kx, wl, 8.0 * wa - DIFF_LAT * scale, -8.0 * wa - DIFF_LAT * scale, wa,
-              2.0 * kx + (1.0 + 2.0 * DIFF_LAT) * scale)
-    for q, plane in enumerate(planes + (jnp.zeros_like(kx),)):
-        for r in range(lat):
-            coef[r + 2, q:q + 1, :] = plane[r:r + 1, :]
-
-    for copy in loads:
-        copy.wait()
-
-    def prepare(r, _):
-        diag[r + 2] = diag[r + 2] * scale + coef[r + 2, 6:7, :]
-        return 0
-
-    lax.fori_loop(0, lat, prepare, 0)
 
     def pack(read, far, n):
         lane = lax.broadcasted_iota(jnp.int32, (n, 128), 1)
@@ -198,11 +169,6 @@
                 to_east = jnp.where(here, pltpu.roll(tail, (68 + 2 * r) % 128, 1), to_east)
         return to_west, to_east
 
-    fixed = [pack(lambda r, cut: diag[r + 2, :, cut], False, channels), pack(lambda r, cut: coef[r + 2, :, cut], False, 8)]
-    for way in range(2):
-        fixed_out[way, 0:channels, :] = fixed[0][way]
-        fixed_out[way, channels:channels + 8, :] = fixed[1][way]
-
     lane = lax.broadcasted_iota(jnp.int32, (channels, 128), 1)
     spot = lax.broadcasted_iota(jnp.int32, (8, 128), 1)
     deep = lax.broadcasted_iota(jnp.int32, (8, 128), 0)
@@ -256,33 +222,36 @@
         def _():
             act(0)
 
-    def send_side(b):
+    def send_all(b):
         k = 2 * b
+        small = jnp.zeros((8, 128), jnp.float32)
+        for up in range(2):
+            for way in range(2):
+                for h in range(channels // 8):
+                    for j in range(2):
+                        at = 16 * up + 8 * way + 4 * h + 2 * j
+                        here = (spot >= at) & (spot < at + 2)
+                        cut = slice(lon - 128, lon) if way else slice(0, 128)
+                        part = basis[k, HALO + (lat - 2 if up else 0) + j, 8 * h:8 * h + 8, cut]
+                        move = (at - (126 if way else 0)) % 128
+                        small = jnp.where(here, pltpu.roll(part, move, 1) if move else part, small)
+        dense = small
+        for g in range(1, 4):
+            moved = pltpu.roll(pltpu.roll(small, 8 - 2 * g, 0), 32 * g, 1)
+            dense = jnp.where(spot // 32 == g, moved, dense)
+        corner_out[b] = dense[0:2, :]
+
+        def go(up):
+            turn_copy(b, up, 0).start()
+            turn_copy(b, up, 1).start()
+            lat_copy(b, up).start()
+
+        each_lat(go)
         to_west, to_east = pack(lambda r, cut: basis[k, r + HALO, :, cut], True, channels)
         side_out[b, 0] = to_west
         side_out[b, 1] = to_east
         lon_copy(b, 0).start()
         lon_copy(b, 1).start()
-        small = jnp.zeros((8, 128), jnp.float32)
-        for up in range(2):
-            for way, ref in enumerate((to_west, to_east)):
-                for h in range(channels // 8):
-                    at = 16 * up + 8 * way + 4 * h
-                    here = (spot >= at) & (spot < at + 4)
-                    start = 2 * lat - 4 if up else 0
-                    part = ref[8 * h:8 * h + 8, :]
-                    small = jnp.where(here, pltpu.roll(part, (at - start) % 128, 1) if at != start else part, small)
-        dense = small
-        for g in range(1, 4):
-            moved = pltpu.roll(pltpu.roll(small, 8 - 2 * g, 0), 32 * g, 1)
-            dense = jnp.where(spot // 32 == g, moved, dense)
-        corner_out[b] = dense[0:2, :]
-
-        def go(up):
-            turn_copy(b, up, 0).start()
-            turn_copy(b, up, 1).start()
-
-        each_lat(go)
 
     def take_corners(b):
         got = jnp.zeros((2, 128), jnp.float32)
@@ -311,23 +280,33 @@
             theta = jnp.where(k == i, jnp.float32(THETA[i] * scale), theta)
         return theta
 
+    def products(k, i, places, acc):
+        n = 0
+        for r in places:
+            prod = basis[k, r + HALO] * basis[i, r + HALO]
+            for h in range(channels // 8):
+                for t in range(tiles):
+                    acc[n % 4] = acc[n % 4] + prod[8 * h:8 * h + 8, 128 * t:128 * t + 128]
+                    n += 1
+        return acc
+
     def dots(k, first, count):
         def one(i, _):
             def part(b, acc):
-                acc = list(acc)
-                for j in range(8):
-                    r = b * 8 + j + HALO + first
-                    prod = basis[k, r] * basis[i, r]
-                    n = 0
-                    for h in range(channels // 8):
-                        for t in range(tiles):
-                            acc[n % 4] = acc[n % 4] + prod[8 * h:8 * h + 8, 128 * t:128 * t + 128]
-                            n += 1
-                return tuple(acc)
+                return tuple(products(k, i, [b * 8 + j + first for j in range(8)], list(acc)))
 
             zero = jnp.zeros((8, 128), jnp.float32)
             acc = lax.fori_loop(0, count // 8, part, (zero,) * 4)
             gram_acc[lax.div(k * (k + 1), 2) + i] = (acc[0] + acc[1]) + (acc[2] + acc[3])
+            return 0
+
+        lax.fori_loop(0, k + 1, one, 0)
+
+    def dots_rest(k):
+        def one(i, _):
+            zero = jnp.zeros((8, 128), jnp.float32)
+            acc = products(k, i, list(range(4)) + list(range(lat - 4, lat)), [zero] * 4)
+            gram_acc[lax.div(k * (k + 1), 2) + i] += (acc[0] + acc[1]) + (acc[2] + acc[3])
             return 0
 
         lax.fori_loop(0, k + 1, one, 0)
@@ -342,7 +321,7 @@
         mixed = lax.dot_general(block[...], split(stack), (((1,), (0,)), ((), ())), preferred_element_type=jnp.float32)
         for j, r in enumerate(picked):
             inside = 0 <= r < lat
-            source = beside[0] if inside else beside[1]
+            source = beside
             left = 2 * r if inside else 64 + 2 * (r % lat)
             right = 64 + 2 * r if inside else 2 * (r % lat)
 
@@ -350,10 +329,14 @@
                 return pltpu.roll(v, shift % 128, 1) if shift % 128 else v
 
             x = [basis[k, r + HALO, :, 128 * t:128 * t + 128] for t in range(tiles)]
-            fwd1 = [pltpu.roll(v, 127, 1) for v in x] + [turn(source, 127 - right)]
-            fwd2 = [pltpu.roll(v, 126, 1) for v in x] + [turn(source, 126 - right)]
-            bwd1 = [turn(source, -left - 1)] + [pltpu.roll(v, 1, 1) for v in x]
-            bwd2 = [turn(source, -left)] + [pltpu.roll(v, 2, 1) for v in x]
+            if source is None:
+                ends = [jnp.zeros_like(lane, jnp.float32)] * 4
+            else:
+                ends = [turn(source, shift) for shift in (127 - right, 126 - right, -left - 1, -left)]
+            fwd1 = [pltpu.roll(v, 127, 1) for v in x] + [ends[0]]
+            fwd2 = [pltpu.roll(v, 126, 1) for v in x] + [ends[1]]
+            bwd1 = [ends[2]] + [pltpu.roll(v, 1, 1) for v in x]
+            bwd2 = [ends[3]] + [pltpu.roll(v, 2, 1) for v in x]
             for t in range(tiles):
                 cut = slice(128 * t, 128 * t + 128)
                 e1 = jnp.where(lane < 127, fwd1[t], fwd1[t + 1])
@@ -388,35 +371,56 @@
         from_east, from_west = side_in[b, 0], side_in[b, 1]
         return jnp.where(lane < 64, from_west, pltpu.roll(from_east, 64, 1))
 
-    def edge_band(b, theta, centre, corners):
+    row = lax.rem(lane, 64) // 2
+    even = lax.rem(lane, 2) == 0
+
+    def edge_coef(q):
+        return jnp.where(spot[0:1] < 64, fixed_in[1, channels + q:channels + q + 1, :],
+                         pltpu.roll(fixed_in[0, channels + q:channels + q + 1, :], 64, 1))
+
+    def edge_band(b, theta, centre):
         from_east, from_west = side_in[b, 0], side_in[b, 1]
         to_west, to_east = side_out[b, 0], side_out[b, 1]
         low = jnp.where(lane < 64, pltpu.roll(from_west, 64, 1), pltpu.roll(to_east, 64, 1))
         high = jnp.where(lane < 64, to_west, from_east)
-        even = lax.rem(lane, 2) == 0
         e1 = jnp.where(even, pltpu.roll(centre, 127, 1), pltpu.roll(high, 1, 1))
         w1 = jnp.where(even, pltpu.roll(low, 127, 1), pltpu.roll(centre, 1, 1))
-        row = lax.rem(lane, 64) // 2
-        n1 = jnp.where(row < lat - 1, pltpu.roll(centre, 126, 1), pltpu.roll(corners, 126, 1))
-        n2 = jnp.where(row < lat - 2, pltpu.roll(centre, 124, 1), pltpu.roll(corners, 124, 1))
-        s1 = jnp.where(row >= 1, pltpu.roll(centre, 2, 1), pltpu.roll(corners, 2, 1))
-        s2 = jnp.where(row >= 2, pltpu.roll(centre, 4, 1), pltpu.roll(corners, 4, 1))
+        n1 = jnp.where(row < lat - 1, pltpu.roll(centre, 126, 1), 0.0)
+        n2 = jnp.where(row < lat - 2, pltpu.roll(centre, 124, 1), 0.0)
+        s1 = jnp.where(row >= 1, pltpu.roll(centre, 2, 1), 0.0)
+        s2 = jnp.where(row >= 2, pltpu.roll(centre, 4, 1), 0.0)
         mixed = lax.dot_general(single[...], split(centre), (((1,), (0,)), ((), ())), preferred_element_type=jnp.float32)
         own = jnp.where(lane < 64, fixed_in[1, 0:channels, :], pltpu.roll(fixed_in[0, 0:channels, :], 64, 1))
-        tail = jnp.where(spot < 64, fixed_in[1, channels:channels + 8, :],
-                         pltpu.roll(fixed_in[0, channels:channels + 8, :], 64, 1))
-
-        def weight(q):
-            return tail[q:q + 1, :]
-
         value = (own - theta) * centre + mixed
-        value = value + (weight(0) * e1 + weight(1) * w1 + weight(2) * (low - high))
-        value = value + weight(3) * n1 + weight(4) * s1 + weight(5) * (s2 - n2)
-        band[...] = value
+        value = value + (edge_coef(0) * e1 + edge_coef(1) * w1 + edge_coef(2) * (low - high))
+        return value + (edge_coef(3) * n1 + edge_coef(4) * s1 + edge_coef(5) * (s2 - n2))
+
+    def edge_turn(corners):
+        n1 = jnp.where(row < lat - 1, 0.0, pltpu.roll(corners, 126, 1))
+        n2 = jnp.where(row < lat - 2, 0.0, pltpu.roll(corners, 124, 1))
+        s1 = jnp.where(row >= 1, 0.0, pltpu.roll(corners, 2, 1))
+        s2 = jnp.where(row >= 2, 0.0, pltpu.roll(corners, 4, 1))
+        return edge_coef(3) * n1 + edge_coef(4) * s1 + edge_coef(5) * (s2 - n2)
+
+    def add_sides(k, centre):
+        def own(q):
+            return jnp.where(spot[0:1] < 64, fixed_out[0, channels + q:channels + q + 1, :],
+                             pltpu.roll(fixed_out[1, channels + q:channels + q + 1, :], 64, 1))
+
+        from_west = own(2) * centre + jnp.where(even, own(1) * pltpu.roll(centre, 127, 1), 0.0)
+        from_east = jnp.where(even, 0.0, own(0) * pltpu.roll(centre, 1, 1)) - own(2) * centre
+        for r in range(lat):
+            left = pltpu.roll(from_west, (128 - 2 * r) % 128, 1) if r else from_west
+            right = pltpu.roll(from_east, (62 - 2 * r) % 128, 1) if 2 * r != 62 else from_east
+            basis[k + 1, r + HALO, :, 0:128] += jnp.where(lane < 2, left, 0.0)
+            basis[k + 1, r + HALO, :, lon - 128:lon] += jnp.where(lane >= 126, right, 0.0)
 
     def stage(b, _):
         k = 2 * b
         theta, after = theta_of(k), theta_of(k + 1)
+        for g in range((lat - 4) // GROUP):
+            rows(k, [2 + GROUP * g + j for j in range(GROUP)], theta, None)
+        rows(k, (0, 1, lat - 2, lat - 1), theta, None, bare=True)
 
         @pl.when(b > 0)
         def _():
@@ -425,28 +429,27 @@
         dots(k, 0, lat)
         lon_copy(b, 0).wait()
         lon_copy(b, 1).wait()
-        centre = middle(b)
-        for g in range((lat - 4) // GROUP):
-            rows(k, [2 + GROUP * g + j for j in range(GROUP)], theta, (centre, None))
-        rows(k, (0, 1, lat - 2, lat - 1), theta, (centre, None), bare=True)
 
         @pl.when(b == 0)
         def _():
             fix_side(0).wait()
             fix_side(1).wait()
 
-        def corners_in(up):
-            turn_copy(b, up, 0).wait_recv()
-            turn_copy(b, up, 1).wait_recv()
-
-        arrive_lat(corners_in)
-        corners = take_corners(b)
-        edge_band(b, theta, centre, corners)
+        centre = middle(b)
+        add_sides(k, centre)
+        band[...] = edge_band(b, theta, centre)
         beside = band[...]
         for g in range((lat - 8) // GROUP):
-            rows(k + 1, [4 + GROUP * g + j for j in range(GROUP)], after, (beside, None))
+            rows(k + 1, [4 + GROUP * g + j for j in range(GROUP)], after, beside)
+
+        @pl.when(b + 1 == BLOCKS)
+        def _():
+            dots(k + 1, 4, lat - 8)
+            dots(k + 2, 4, lat - 8)
 
         def halo_in(way):
+            turn_copy(b, way, 0).wait_recv()
+            turn_copy(b, way, 1).wait_recv()
             lat_copy(b, way).wait_recv()
 
             @pl.when(b == 0)
@@ -455,19 +458,20 @@
                     copy.wait_recv()
 
         arrive_lat(halo_in)
-        rows(k, (-2, -1, lat, lat + 1), theta, (None, corners))
+        corners = take_corners(b)
+        beside = band[...] + edge_turn(corners)
+        rows(k, (-2, -1, lat, lat + 1), theta, corners)
         south, north = basis[k, HALO - 1], basis[k, HALO + lat]
         basis[k + 1, HALO] += coef[2, 4:5, :] * south + coef[2, 5:6, :] * basis[k, HALO - 2]
         basis[k + 1, HALO + 1] += coef[3, 5:6, :] * south
         basis[k + 1, HALO + lat - 1] += coef[lat + 1, 3:4, :] * north - coef[lat + 1, 5:6, :] * basis[k, HALO + lat + 1]
         basis[k + 1, HALO + lat - 2] -= coef[lat, 5:6, :] * north
-        rows(k + 1, tuple(range(4)), after, (beside, None))
-        rows(k + 1, tuple(range(lat - 4, lat)), after, (beside, None))
+        rows(k + 1, tuple(range(4)), after, beside)
+        rows(k + 1, tuple(range(lat - 4, lat)), after, beside)
 
         @pl.when(b + 1 < BLOCKS)
         def _():
-            each_lat(lambda way: lat_copy(b + 1, way).start())
-            send_side(b + 1)
+            send_all(b + 1)
 
         def sent(way):
             lat_copy(b, way).wait_send()
@@ -482,20 +486,53 @@
         each_lat(sent)
         return 0
 
+    for copy in loads[0]:
+        copy.wait()
     pl.semaphore_wait(barrier, total - 1)
-    each_lat(lambda way: lat_copy(0, way).start())
-    send_side(0)
-    fix_side(0).start()
-    fix_side(1).start()
+    send_all(0)
+    for copy in small:
+        copy.wait()
+    place = (lax.broadcasted_iota(jnp.int32, (lat, 128), 0) + iy * lat).astype(jnp.float32)
+    phi = -math.pi / 2 + (place + 0.5) * (math.pi / (lat * ny))
+    kx = (DIFF_LON * scale) / (jnp.cos(phi) ** 2 + 0.1)
+    wl = wl_ref[...] * (scale / 12.0)
+    wa = wa_ref[...] * (scale / 12.0)
+    kx = jnp.concatenate([kx] * tiles, axis=1)
+    planes = (8.0 * wl - kx, -8.0 * wl - kx, wl, 8.0 * wa - DIFF_LAT * scale, -8.0 * wa - DIFF_LAT * scale, wa,
+              2.0 * kx + (1.0 + 2.0 * DIFF_LAT) * scale)
+    for q, plane in enumerate(planes + (jnp.zeros_like(kx),)):
+        for r in range(lat):
+            coef[r + 2, q:q + 1, :] = plane[r:r + 1, :]
+
+    for copy in loads[1]:
+        copy.wait()
+
+    def prepare(r, _):
+        diag[r + 2] = diag[r + 2] * scale + coef[r + 2, 6:7, :]
+        return 0
+
+    lax.fori_loop(0, lat, prepare, 0)
 
     def give_fixed(way):
         for copy in fix_copies(way):
             copy.start()
 
     each_lat(give_fixed)
+    fixed = [pack(lambda r, cut: diag[r + 2, :, cut], False, channels), pack(lambda r, cut: coef[r + 2, :, cut], False, 8)]
+    for way in range(2):
+        fixed_out[way, 0:channels, :] = fixed[0][way]
+        fixed_out[way, channels:channels + 8, :] = fixed[1][way]
+    fix_side(0).start()
+    fix_side(1).start()
+    single[...] = widen(c_ref[...], channels)[0].astype(jnp.bfloat16)
+    tall = lax.dot_general(spread(size), c_ref[...], (((1,), (0,)), ((), ())), precision=HI,
+                           preferred_element_type=jnp.float32)
+    wide, across = widen(tall, size)
+    down = lax.broadcasted_iota(jnp.int32, (size, 3 * size), 0)
+    block[...] = jnp.where(down // channels == lax.rem(across, size) // channels, wide, 0.0).astype(jnp.bfloat16)
     lax.fori_loop(0, BLOCKS, stage, 0)
-    dots(ITERS - 1, 0, lat)
-    dots(ITERS, 0, lat)
+    dots_rest(ITERS - 1)
+    dots_rest(ITERS)
 
     sums = jnp.concatenate(
         [jnp.sum(gram_acc[n], axis=0, keepdims=True) for n in range(len(PAIRS))]
@@ -589,7 +626,7 @@
         basis, weights = pl.pallas_call(
             functools.partial(kernel, nx, ny),
             out_shape=(pltpu.VMEM((ITERS + 1, lat + 2 * HALO, channels, lon), f32), pltpu.VMEM((2 * ITERS + 1, 8, 128), f32)),
-            in_specs=[hbm, hbm, vmem, hbm, hbm],
+            in_specs=[hbm] * 5,
             out_specs=(vmem, vmem),
             scratch_shapes=[
                 pltpu.VMEM((lat + 4, channels, lon), f32),
@@ -606,15 +643,15 @@
                 pltpu.VMEM((len(PAIRS), 8, 128), f32),
                 pltpu.VMEM((1, 128), f32),
                 pltpu.VMEM((nx * ny, 1, 128), f32),
-                pltpu.VMEM((lat, lon), f32), pltpu.VMEM((lat, lon), f32),
-                dma((2, channels)), dma((2,)),
+                pltpu.VMEM((channels, channels), f32), pltpu.VMEM((lat, lon), f32), pltpu.VMEM((lat, lon), f32),
+                dma((2, channels)), dma((3,)),
                 dma((BLOCKS, 2)), dma((BLOCKS, 2)), dma((BLOCKS, 2)), dma((BLOCKS, 2)),
                 dma((BLOCKS, 4)), dma((BLOCKS, 4)), dma((3, 2)), dma((3, 2)),
                 dma((nx * ny,)), dma((nx * ny,)),
             ],
             compiler_params=pltpu.CompilerParams(
                 collective_id=0, has_side_effects=True, vmem_limit_bytes=24 * 1024 * 1024),
-        )(keep(forcing), keep(damping), coupling, keep(wind_lon), keep(wind_lat))
+        )(*map(keep, (forcing, damping, coupling, wind_lon, wind_lat)))
         shape = jax.ShapeDtypeStruct((channels, lat, lon), f32)
         return pl.pallas_call(
             finish,

time: 45.4 us -> 40.8 us (0.90)
  Pallas kernels: 43.9 us -> 40 us
  local copies, waits for them, and re-layouts: 0.69 us -> 0 us
    pallas_call x1, Pallas kernels: 40.7 us -> 36.9 us  [per_device(): pl.pallas_call(functools.partial(kernel, nx, ny), out_shape=(pltpu.VMEM((...]
    unnamed x2 -> x0, local copies, waits for them, and re-layouts: 0.69 us -> none
where the time goes in v1:
time: 40.8 us; the launch traced here: 40.6 us
  Pallas kernels  40 us (98%)
  between operations  0.64 us (2%)
    pallas_call x1, Pallas kernels, per_device(): pl.pallas_call(functools.partial(kernel, nx, ny), out_shape=(pltpu.VMEM((...  36.9 us
    pallas_call x1, Pallas kernels, per_device(): pl.pallas_call(finish, out_shape=(shape, shape), in_specs=[vmem, vmem], o...  3.11 us

profile of v1, /device:TPU:0, one launch (start us, length us, event | category | flops | bytes accessed | tf_op | source)
XLA Modules:
  0.0 40.6 jit_solution(3134996150724165127)
XLA Ops:
  0.6 36.9 %shard_map.68 = (f32[9,40,16,256]{3,2,1,0:T(8,128)S(1)}, f32[17,8,128]{2,1,0:T(8,128)S(1)}) custom-call(f32[16,32,256]{2,1,0:T(8,128)} %f_hbm.1, f32[16,32,256]{2,1,0:T(8,128)} %d_hbm.1, f32[16,16]{1,0:T(8,128)} %c_hbm.1, f32[32,256]{1,0:T(8,128)} %wl_hbm.1, f32[32,256]{1,0:T(8,128)} %wa_hbm.1), custom_call_target="tpu_custom_call" | custom-call | tf_op jit(solution)/shard_map/pallas_call | solution.py:626
  37.5 3.1 %shard_map.69 = (f32[16,32,256]{2,1,0:T(8,128)}, f32[16,32,256]{2,1,0:T(8,128)}) custom-call(f32[9,40,16,256]{3,2,1,0:T(8,128)S(1)} %get-tuple-element.4.b_ref, f32[17,8,128]{2,1,0:T(8,128)S(1)} %get-tuple-element.5.w_ref), custom_call_target="tpu_custom_call" | custom-call | tf_op jit(solution)/shard_map/pallas_call | solution.py:656

commit v2 on v1

--- a/solution.py
+++ b/solution.py
@@ -92,10 +92,45 @@
     return answer, apply_to(answer)
 
 
+def word_plan(nx, ny):
+    def doubled(n):
+        out = [2]
+        while out[-1] < n:
+            out.append(2 * out[-1])
+        return out[:-1]
+
+    far_lat, far_lon = doubled(ny), doubled(nx // 2 + 1)
+    words = max(len(far_lat), len(far_lon))
+    reach = {}
+    for x in range(nx):
+        for y in range(ny):
+            reach[x, y] = {((x + dx) % nx, y + dy) for dx in (-1, 0, 1) for dy in (-1, 0, 1) if 0 <= y + dy < ny}
+    near = {place: set(known) for place, known in reach.items()}
+
+    def peers(x, y, n):
+        out = []
+        if n < len(far_lat):
+            out += [(x, y + d) for d in (-far_lat[n], far_lat[n]) if 0 <= y + d < ny]
+        if n < len(far_lon):
+            out += [((x + d) % nx, y) for d in (-far_lon[n], far_lon[n])]
+        return out
+
+    told = None
+    for n in range(BLOCKS):
+        before = reach
+        reach = {place: set().union(*(before[other] for other in near[place])) for place in before}
+        if told is not None:
+            reach = {place: known.union(*(told[other] for other in peers(*place, n - 1))) for place, known in reach.items()}
+        told = reach
+    if any(len(known) < nx * ny for known in reach.values()):
+        far_lon = far_lon + [nx // 2] * (max(BLOCKS, words + 1) - len(far_lon))
+    return far_lat, far_lon
+
+
 def kernel(nx, ny, f_hbm, d_hbm, c_hbm, wl_hbm, wa_hbm, basis, splats,
            diag, coef, block, single, side_in, side_out, band, fixed_in, fixed_out, corner_in, corner_out,
-           gram_acc, mine, slots, c_ref, wl_ref, wa_ref,
-           in_sem, wind_sem, lat_send, lat_recv, lon_send, lon_recv, turn_send, turn_recv, fix_send, fix_recv, red_send, red_recv):
+           gram_acc, mine, slots, c_ref, wl_ref, wa_ref, wind_in, kx_in, turned,
+           in_sem, wind_sem, lat_send, lat_recv, lon_send, lon_recv, turn_send, turn_recv, fix_send, fix_recv, red_send, red_recv, word):
     channels, lat, lon = f_hbm.shape
     tiles = lon // 128
     total = nx * ny
@@ -103,25 +138,64 @@
     me = ix * ny + iy
     east, west = lax.rem(ix + 1, nx), lax.rem(ix + nx - 1, nx)
 
+    small = [pltpu.make_async_copy(src, dst, wind_sem.at[n])
+             for n, (src, dst) in enumerate(((wl_hbm, wl_ref), (wa_hbm, wa_ref), (c_hbm, c_ref)))]
+    for copy in small:
+        copy.start()
     loads = [[], []]
     for q, (src, dst, off) in enumerate(((f_hbm, basis.at[0], HALO), (d_hbm, diag, 2))):
         for c in range(channels):
             copy = pltpu.make_async_copy(src.at[c], dst.at[pl.ds(off, lat), c, :], in_sem.at[q, c])
             copy.start()
             loads[q].append(copy)
-    small = [pltpu.make_async_copy(src, dst, wind_sem.at[n])
-             for n, (src, dst) in enumerate(((wl_hbm, wl_ref), (wa_hbm, wa_ref), (c_hbm, c_ref)))]
-    for copy in small:
-        copy.start()
 
     barrier = pltpu.get_barrier_semaphore()
 
-    def greet(o, _):
-        other = lax.rem(me + o, total)
-        pl.semaphore_signal(barrier, inc=1, device_id=(other // ny, lax.rem(other, ny)), device_id_type=MESH)
-        return 0
-
-    lax.fori_loop(1, total, greet, 0)
+    def greet(to, sem=barrier):
+        pl.semaphore_signal(sem, inc=1, device_id=to, device_id_type=MESH)
+
+    greet((east, iy))
+    greet((west, iy))
+
+    def greet_lat(to):
+        greet((ix, to))
+        greet((east, to))
+        greet((west, to))
+
+    @pl.when(iy > 0)
+    def _():
+        greet_lat(iy - 1)
+
+    @pl.when(iy < ny - 1)
+    def _():
+        greet_lat(iy + 1)
+
+    far_lat, far_lon = word_plan(nx, ny)
+
+    def spread_word(n):
+        if n < len(far_lat):
+            d = far_lat[n]
+
+            @pl.when(iy >= d)
+            def _():
+                greet((ix, iy - d), word.at[n])
+
+            @pl.when(iy + d < ny)
+            def _():
+                greet((ix, iy + d), word.at[n])
+
+        if n < len(far_lon):
+            greet((lax.rem(ix + far_lon[n], nx), iy), word.at[n])
+            greet((lax.rem(ix + nx - far_lon[n], nx), iy), word.at[n])
+
+    def hear_word(n):
+        count = 2 if n < len(far_lon) else 0
+        if n < len(far_lat):
+            d = far_lat[n]
+            count = count + jnp.where(iy >= d, 1, 0) + jnp.where(iy + d < ny, 1, 0)
+        pl.semaphore_wait(word.at[n], count)
+
+    words = max(len(far_lat), len(far_lon))
 
     scale = 1.0 / WIDTH
     size = GROUP * channels
@@ -153,6 +227,15 @@
     @pl.when(iy == ny - 1)
     def _():
         blank(1)
+
+    def fill_coef(wl, wa, kx, at):
+        wl, wa = wl * (scale / 12.0), wa * (scale / 12.0)
+        kx = jnp.concatenate([kx] * tiles, axis=1)
+        planes = (8.0 * wl - kx, -8.0 * wl - kx, wl, 8.0 * wa - DIFF_LAT * scale, -8.0 * wa - DIFF_LAT * scale, wa,
+                  2.0 * kx + (1.0 + 2.0 * DIFF_LAT) * scale, jnp.zeros_like(kx))
+        for q, plane in enumerate(planes):
+            for r in range(wl.shape[0]):
+                coef[r + at, q:q + 1, :] = plane[r:r + 1, :]
 
     def pack(read, far, n):
         lane = lax.broadcasted_iota(jnp.int32, (n, 128), 1)
@@ -180,19 +263,26 @@
     def lat_to(way):
         return iy + 1 if way else iy - 1
 
-    def lat_copy(b, way):
-        src = pl.ds(lat, HALO) if way else pl.ds(HALO, HALO)
-        dst = pl.ds(0, HALO) if way else pl.ds(lat + HALO, HALO)
-        return copy_to(basis.at[2 * b, src], basis.at[2 * b, dst], lat_send.at[b, way], lat_recv.at[b, way], (ix, lat_to(way)))
-
-    def fix_copies(way):
+    def lat_copy(b, way, near):
+        if way:
+            src, dst = HALO + lat - (2 if near else 4), 2 if near else 0
+        else:
+            src, dst = HALO + (0 if near else 2), HALO + lat + (0 if near else 2)
+        return copy_to(basis.at[2 * b, pl.ds(src, 2)], basis.at[2 * b, pl.ds(dst, 2)], lat_send.at[b, way, near],
+                       lat_recv.at[b, way, near], (ix, lat_to(way)))
+
+    def diag_copy(way):
         src = pl.ds(lat, 2) if way else pl.ds(2, 2)
         dst = pl.ds(0, 2) if way else pl.ds(lat + 2, 2)
-        return [copy_to(ref.at[src], ref.at[dst], fix_send.at[n, way], fix_recv.at[n, way], (ix, lat_to(way)))
-                for n, ref in enumerate((diag, coef))]
+        return copy_to(diag.at[src], diag.at[dst], fix_send.at[0, way], fix_recv.at[0, way], (ix, lat_to(way)))
+
+    def wind_copies(way):
+        src = pl.ds(lat - 2, 2) if way else pl.ds(0, 2)
+        return [copy_to(ref.at[src], wind_in.at[n, way], fix_send.at[1 + n, way], fix_recv.at[1 + n, way], (ix, lat_to(way)))
+                for n, ref in enumerate((wl_ref, wa_ref))]
 
     def fix_side(way):
-        return copy_to(fixed_out.at[way], fixed_in.at[way], fix_send.at[2, way], fix_recv.at[2, way],
+        return copy_to(fixed_out.at[way], fixed_in.at[way], fix_send.at[3, way], fix_recv.at[3, way],
                        (east if way else west, iy))
 
     def lon_copy(b, way):
@@ -222,7 +312,7 @@
         def _():
             act(0)
 
-    def send_all(b):
+    def send_corners(b):
         k = 2 * b
         small = jnp.zeros((8, 128), jnp.float32)
         for up in range(2):
@@ -244,9 +334,11 @@
         def go(up):
             turn_copy(b, up, 0).start()
             turn_copy(b, up, 1).start()
-            lat_copy(b, up).start()
 
         each_lat(go)
+
+    def send_sides(b):
+        k = 2 * b
         to_west, to_east = pack(lambda r, cut: basis[k, r + HALO, :, cut], True, channels)
         side_out[b, 0] = to_west
         side_out[b, 1] = to_east
@@ -302,14 +394,20 @@
 
         lax.fori_loop(0, k + 1, one, 0)
 
-    def dots_rest(k):
+    def dots_rest():
+        picked = list(range(4)) + list(range(lat - 4, lat))
+        zero = jnp.zeros((8, 128), jnp.float32)
+
+        def save(k, i, acc):
+            gram_acc[k * (k + 1) // 2 + i] += (acc[0] + acc[1]) + (acc[2] + acc[3])
+
         def one(i, _):
-            zero = jnp.zeros((8, 128), jnp.float32)
-            acc = products(k, i, list(range(4)) + list(range(lat - 4, lat)), [zero] * 4)
-            gram_acc[lax.div(k * (k + 1), 2) + i] += (acc[0] + acc[1]) + (acc[2] + acc[3])
+            for k in (ITERS - 1, ITERS):
+                save(k, i, products(k, i, picked, [zero] * 4))
             return 0
 
-        lax.fori_loop(0, k + 1, one, 0)
+        lax.fori_loop(0, ITERS, one, 0)
+        save(ITERS, ITERS, products(ITERS, ITERS, picked, [zero] * 4))
 
     def split(stack):
         high = stack.astype(jnp.bfloat16)
@@ -447,40 +545,71 @@
             dots(k + 1, 4, lat - 8)
             dots(k + 2, 4, lat - 8)
 
-        def halo_in(way):
+        def corners_in(way):
             turn_copy(b, way, 0).wait_recv()
             turn_copy(b, way, 1).wait_recv()
-            lat_copy(b, way).wait_recv()
 
             @pl.when(b == 0)
             def _():
-                for copy in fix_copies(way):
+                for copy in wind_copies(way):
                     copy.wait_recv()
-
-        arrive_lat(halo_in)
-        corners = take_corners(b)
-        beside = band[...] + edge_turn(corners)
-        rows(k, (-2, -1, lat, lat + 1), theta, corners)
+                fill_coef(wind_in[0, way], wind_in[1, way], kx_in[way, 6:8] if way else kx_in[way, 0:2], 0 if way else lat + 2)
+
+        arrive_lat(corners_in)
+        turned[0] = take_corners(b)
+        turned[1] = band[...] + edge_turn(turned[0])
+        arrive_lat(lambda way: lat_copy(b, way, 1).wait_recv())
+        beside = turned[1]
         south, north = basis[k, HALO - 1], basis[k, HALO + lat]
         basis[k + 1, HALO] += coef[2, 4:5, :] * south + coef[2, 5:6, :] * basis[k, HALO - 2]
         basis[k + 1, HALO + 1] += coef[3, 5:6, :] * south
         basis[k + 1, HALO + lat - 1] += coef[lat + 1, 3:4, :] * north - coef[lat + 1, 5:6, :] * basis[k, HALO + lat + 1]
         basis[k + 1, HALO + lat - 2] -= coef[lat, 5:6, :] * north
-        rows(k + 1, tuple(range(4)), after, beside)
-        rows(k + 1, tuple(range(lat - 4, lat)), after, beside)
-
-        @pl.when(b + 1 < BLOCKS)
+        rows(k + 1, (2, 3, lat - 4, lat - 3), after, beside)
+        more = b + 1 < BLOCKS
+
+        @pl.when(more)
         def _():
-            send_all(b + 1)
+            each_lat(lambda way: lat_copy(b + 1, way, 0).start())
+
+        def far_in(way):
+            lat_copy(b, way, 0).wait_recv()
+
+            @pl.when(b == 0)
+            def _():
+                diag_copy(way).wait_recv()
+
+        arrive_lat(far_in)
+        rows(k, (-2, -1, lat, lat + 1), theta, turned[0])
+        rows(k + 1, (0, 1, lat - 2, lat - 1), after, turned[1])
+
+        @pl.when(more)
+        def _():
+            send_corners(b + 1)
+            each_lat(lambda way: lat_copy(b + 1, way, 1).start())
+            send_sides(b + 1)
+
+        for n in range(min(words, BLOCKS)):
+            @pl.when(b == n)
+            def _():
+                if n:
+                    hear_word(n - 1)
+                spread_word(n)
+
+        if words < BLOCKS:
+            @pl.when(b == words)
+            def _():
+                hear_word(words - 1)
 
         def sent(way):
-            lat_copy(b, way).wait_send()
+            lat_copy(b, way, 0).wait_send()
+            lat_copy(b, way, 1).wait_send()
             turn_copy(b, way, 0).wait_send()
             turn_copy(b, way, 1).wait_send()
 
             @pl.when(b == 0)
             def _():
-                for copy in fix_copies(way):
+                for copy in wind_copies(way) + [diag_copy(way)]:
                     copy.wait_send()
 
         each_lat(sent)
@@ -488,22 +617,29 @@
 
     for copy in loads[0]:
         copy.wait()
-    pl.semaphore_wait(barrier, total - 1)
-    send_all(0)
+    pl.semaphore_wait(barrier, 2 + jnp.where(iy > 0, 3, 0) + jnp.where(iy < ny - 1, 3, 0))
+    send_corners(0)
+
+    def first_rows(way):
+        lat_copy(0, way, 1).start()
+        lat_copy(0, way, 0).start()
+
+    each_lat(first_rows)
+    send_sides(0)
     for copy in small:
         copy.wait()
-    place = (lax.broadcasted_iota(jnp.int32, (lat, 128), 0) + iy * lat).astype(jnp.float32)
+
+    def first_winds(way):
+        for copy in wind_copies(way):
+            copy.start()
+
+    each_lat(first_winds)
+    place = (lax.broadcasted_iota(jnp.int32, (lat + 16, 128), 0) + iy * lat - 8).astype(jnp.float32)
     phi = -math.pi / 2 + (place + 0.5) * (math.pi / (lat * ny))
     kx = (DIFF_LON * scale) / (jnp.cos(phi) ** 2 + 0.1)
-    wl = wl_ref[...] * (scale / 12.0)
-    wa = wa_ref[...] * (scale / 12.0)
-    kx = jnp.concatenate([kx] * tiles, axis=1)
-    planes = (8.0 * wl - kx, -8.0 * wl - kx, wl, 8.0 * wa - DIFF_LAT * scale, -8.0 * wa - DIFF_LAT * scale, wa,
-              2.0 * kx + (1.0 + 2.0 * DIFF_LAT) * scale)
-    for q, plane in enumerate(planes + (jnp.zeros_like(kx),)):
-        for r in range(lat):
-            coef[r + 2, q:q + 1, :] = plane[r:r + 1, :]
-
+    kx_in[0] = kx[lat + 8:lat + 16]
+    kx_in[1] = kx[0:8]
+    fill_coef(wl_ref[...], wa_ref[...], kx[8:lat + 8], 2)
     for copy in loads[1]:
         copy.wait()
 
@@ -511,13 +647,10 @@
         diag[r + 2] = diag[r + 2] * scale + coef[r + 2, 6:7, :]
         return 0
 
-    lax.fori_loop(0, lat, prepare, 0)
-
-    def give_fixed(way):
-        for copy in fix_copies(way):
-            copy.start()
-
-    each_lat(give_fixed)
+    for r in (0, 1, lat - 2, lat - 1):
+        prepare(r, 0)
+    each_lat(lambda way: diag_copy(way).start())
+    lax.fori_loop(2, lat - 2, prepare, 0)
     fixed = [pack(lambda r, cut: diag[r + 2, :, cut], False, channels), pack(lambda r, cut: coef[r + 2, :, cut], False, 8)]
     for way in range(2):
         fixed_out[way, 0:channels, :] = fixed[0][way]
@@ -531,8 +664,11 @@
     down = lax.broadcasted_iota(jnp.int32, (size, 3 * size), 0)
     block[...] = jnp.where(down // channels == lax.rem(across, size) // channels, wide, 0.0).astype(jnp.bfloat16)
     lax.fori_loop(0, BLOCKS, stage, 0)
-    dots_rest(ITERS - 1)
-    dots_rest(ITERS)
+    for n in range(BLOCKS, words + 1):
+        hear_word(n - 1)
+        if n < words:
+            spread_word(n)
+    dots_rest()
 
     sums = jnp.concatenate(
         [jnp.sum(gram_acc[n], axis=0, keepdims=True) for n in range(len(PAIRS))]
@@ -644,10 +780,11 @@
                 pltpu.VMEM((1, 128), f32),
                 pltpu.VMEM((nx * ny, 1, 128), f32),
                 pltpu.VMEM((channels, channels), f32), pltpu.VMEM((lat, lon), f32), pltpu.VMEM((lat, lon), f32),
+                pltpu.VMEM((2, 2, 2, lon), f32), pltpu.VMEM((2, 8, 128), f32), pltpu.VMEM((2, channels, 128), f32),
                 dma((2, channels)), dma((3,)),
-                dma((BLOCKS, 2)), dma((BLOCKS, 2)), dma((BLOCKS, 2)), dma((BLOCKS, 2)),
-                dma((BLOCKS, 4)), dma((BLOCKS, 4)), dma((3, 2)), dma((3, 2)),
-                dma((nx * ny,)), dma((nx * ny,)),
+                dma((BLOCKS, 2, 2)), dma((BLOCKS, 2, 2)), dma((BLOCKS, 2)), dma((BLOCKS, 2)),
+                dma((BLOCKS, 4)), dma((BLOCKS, 4)), dma((4, 2)), dma((4, 2)),
+                dma((nx * ny,)), dma((nx * ny,)), pltpu.SemaphoreType.REGULAR((8,)),
             ],
             compiler_params=pltpu.CompilerParams(
                 collective_id=0, has_side_effects=True, vmem_limit_bytes=24 * 1024 * 1024),

time: 40.8 us -> 39.2 us (0.961)
  Pallas kernels: 40 us -> 38.3 us
    pallas_call x1, Pallas kernels: 36.9 us -> 35.2 us  [per_device(): pl.pallas_call(functools.partial(kernel, nx, ny), out_shape=(pltpu.VMEM((...]
where the time goes in v2:
time: 39.2 us; the launch traced here: 39 us
  Pallas kernels  38.3 us (98%)
  between operations  0.64 us (2%)
    pallas_call x1, Pallas kernels, per_device(): pl.pallas_call(functools.partial(kernel, nx, ny), out_shape=(pltpu.VMEM((...  35.2 us
    pallas_call x1, Pallas kernels, per_device(): pl.pallas_call(finish, out_shape=(shape, shape), in_specs=[vmem, vmem], o...  3.11 us

profile of v2, /device:TPU:0, one launch (start us, length us, event | category | flops | bytes accessed | tf_op | source)
XLA Modules:
  0.0 39.0 jit_solution(14482854380371498306)
XLA Ops:
  0.6 35.2 %shard_map.68 = (f32[9,40,16,256]{3,2,1,0:T(8,128)S(1)}, f32[17,8,128]{2,1,0:T(8,128)S(1)}) custom-call(f32[16,32,256]{2,1,0:T(8,128)} %f_hbm.1, f32[16,32,256]{2,1,0:T(8,128)} %d_hbm.1, f32[16,16]{1,0:T(8,128)} %c_hbm.1, f32[32,256]{1,0:T(8,128)} %wl_hbm.1, f32[32,256]{1,0:T(8,128)} %wa_hbm.1), custom_call_target="tpu_custom_call" | custom-call | tf_op jit(solution)/shard_map/pallas_call | solution.py:762
  35.8 3.1 %shard_map.69 = (f32[16,32,256]{2,1,0:T(8,128)}, f32[16,32,256]{2,1,0:T(8,128)}) custom-call(f32[9,40,16,256]{3,2,1,0:T(8,128)S(1)} %get-tuple-element.4.b_ref, f32[17,8,128]{2,1,0:T(8,128)S(1)} %get-tuple-element.5.w_ref), custom_call_target="tpu_custom_call" | custom-call | tf_op jit(solution)/shard_map/pallas_call | solution.py:793

commit v3 on v2

--- a/solution.py
+++ b/solution.py
@@ -33,6 +33,12 @@
         out[k] = low if out[k] is None else out[k] + low
         out[k + 1] = WIDTH * value
     return out
+
+
+def tree(terms):
+    while len(terms) > 1:
+        terms = [a + b for a, b in zip(terms[::2], terms[1::2])] + ([terms[-1]] if len(terms) % 2 else [])
+    return terms[0]
 
 
 def small_solve(gram):
@@ -129,7 +135,7 @@
 
 def kernel(nx, ny, f_hbm, d_hbm, c_hbm, wl_hbm, wa_hbm, basis, splats,
            diag, coef, block, single, side_in, side_out, band, fixed_in, fixed_out, corner_in, corner_out,
-           gram_acc, mine, slots, c_ref, wl_ref, wa_ref, wind_in, kx_in, turned,
+           gram_acc, slots, c_ref, wl_ref, wa_ref, wind_in, kx_in, turned,
            in_sem, wind_sem, lat_send, lat_recv, lon_send, lon_recv, turn_send, turn_recv, fix_send, fix_recv, red_send, red_recv, word):
     channels, lat, lon = f_hbm.shape
     tiles = lon // 128
@@ -237,10 +243,10 @@
             for r in range(wl.shape[0]):
                 coef[r + at, q:q + 1, :] = plane[r:r + 1, :]
 
-    def pack(read, far, n):
+    def pack(read, far, n, picked=None):
         lane = lax.broadcasted_iota(jnp.int32, (n, 128), 1)
         to_west = to_east = jnp.zeros((n, 128), jnp.float32)
-        for r in range(lat):
+        for r in picked or range(lat):
             head = read(r, slice(0, 128))
             tail = read(r, slice(lon - 128, lon))
             here = (lane >= 2 * r) & (lane < 2 * r + 2)
@@ -285,9 +291,11 @@
         return copy_to(fixed_out.at[way], fixed_in.at[way], fix_send.at[3, way], fix_recv.at[3, way],
                        (east if way else west, iy))
 
-    def lon_copy(b, way):
-        return copy_to(side_out.at[b, way], side_in.at[b, way], lon_send.at[b, way], lon_recv.at[b, way],
-                       (east if way else west, iy))
+    def lon_copy(b, part, way):
+        return copy_to(side_out.at[b, part, way], side_in.at[b, part, way], lon_send.at[b, part, way],
+                       lon_recv.at[b, part, way], (east if way else west, iy))
+
+    sided = (list(range(4, lat - 4)), list(range(4)) + list(range(lat - 4, lat)))
 
     def turn_copy(b, up, way):
         n = 2 * up + way
@@ -337,13 +345,13 @@
 
         each_lat(go)
 
-    def send_sides(b):
+    def send_sides(b, part):
         k = 2 * b
-        to_west, to_east = pack(lambda r, cut: basis[k, r + HALO, :, cut], True, channels)
-        side_out[b, 0] = to_west
-        side_out[b, 1] = to_east
-        lon_copy(b, 0).start()
-        lon_copy(b, 1).start()
+        to_west, to_east = pack(lambda r, cut: basis[k, r + HALO, :, cut], True, channels, sided[part])
+        side_out[b, part, 0] = to_west
+        side_out[b, part, 1] = to_east
+        lon_copy(b, part, 0).start()
+        lon_copy(b, part, 1).start()
 
     def take_corners(b):
         got = jnp.zeros((2, 128), jnp.float32)
@@ -372,42 +380,48 @@
             theta = jnp.where(k == i, jnp.float32(THETA[i] * scale), theta)
         return theta
 
-    def products(k, i, places, acc):
-        n = 0
+    def products(pairs, places, accs):
         for r in places:
-            prod = basis[k, r + HALO] * basis[i, r + HALO]
             for h in range(channels // 8):
                 for t in range(tiles):
-                    acc[n % 4] = acc[n % 4] + prod[8 * h:8 * h + 8, 128 * t:128 * t + 128]
-                    n += 1
-        return acc
-
-    def dots(k, first, count):
+                    at = (r + HALO, slice(8 * h, 8 * h + 8), slice(128 * t, 128 * t + 128))
+                    held = {}
+
+                    def read(k):
+                        if id(k) not in held:
+                            held[id(k)] = basis[(k,) + at]
+                        return held[id(k)]
+
+                    for n, (k, i) in enumerate(pairs):
+                        m = (2 * h + t) % 2
+                        accs[2 * n + m] = accs[2 * n + m] + read(k) * read(i)
+        return accs
+
+    def keep(k, i, acc, more):
+        at = lax.div(k * (k + 1), 2) + i
+        gram_acc[at] = gram_acc[at] + acc if more else acc
+
+    def dots(pairs, first, count, more=False):
+        zero = jnp.zeros((8, 128), jnp.float32)
+        if count == 8:
+            accs = products(pairs, [(j + first) % lat for j in range(8)],
+                            [zero] * (2 * len(pairs)))
+        else:
+            def part(b, accs):
+                return tuple(products(pairs, [b * 8 + j + first for j in range(8)], list(accs)))
+
+            accs = lax.fori_loop(0, count // 8, part, (zero,) * (2 * len(pairs)))
+        for n, (k, i) in enumerate(pairs):
+            keep(k, i, accs[2 * n] + accs[2 * n + 1], more)
+
+    def dots_two(k, first, count, more=False):
         def one(i, _):
-            def part(b, acc):
-                return tuple(products(k, i, [b * 8 + j + first for j in range(8)], list(acc)))
-
-            zero = jnp.zeros((8, 128), jnp.float32)
-            acc = lax.fori_loop(0, count // 8, part, (zero,) * 4)
-            gram_acc[lax.div(k * (k + 1), 2) + i] = (acc[0] + acc[1]) + (acc[2] + acc[3])
+            before = k - 1
+            dots([(before, i), (k, i)], first, count, more)
             return 0
 
-        lax.fori_loop(0, k + 1, one, 0)
-
-    def dots_rest():
-        picked = list(range(4)) + list(range(lat - 4, lat))
-        zero = jnp.zeros((8, 128), jnp.float32)
-
-        def save(k, i, acc):
-            gram_acc[k * (k + 1) // 2 + i] += (acc[0] + acc[1]) + (acc[2] + acc[3])
-
-        def one(i, _):
-            for k in (ITERS - 1, ITERS):
-                save(k, i, products(k, i, picked, [zero] * 4))
-            return 0
-
-        lax.fori_loop(0, ITERS, one, 0)
-        save(ITERS, ITERS, products(ITERS, ITERS, picked, [zero] * 4))
+        lax.fori_loop(0, k, one, 0)
+        dots([(k, k)], first, count, more)
 
     def split(stack):
         high = stack.astype(jnp.bfloat16)
@@ -465,9 +479,11 @@
                     value = value + weight(5) * near(-2)
                 basis[k + 1, r + HALO, :, cut] = value
 
-    def middle(b):
-        from_east, from_west = side_in[b, 0], side_in[b, 1]
-        return jnp.where(lane < 64, from_west, pltpu.roll(from_east, 64, 1))
+    def middle(got):
+        return jnp.where(lane < 64, got[1], pltpu.roll(got[0], 64, 1))
+
+    def both(ref, b, part):
+        return [ref[b, 0, way] + ref[b, 1, way] if part else ref[b, 0, way] for way in range(2)]
 
     row = lax.rem(lane, 64) // 2
     even = lax.rem(lane, 2) == 0
@@ -476,9 +492,9 @@
         return jnp.where(spot[0:1] < 64, fixed_in[1, channels + q:channels + q + 1, :],
                          pltpu.roll(fixed_in[0, channels + q:channels + q + 1, :], 64, 1))
 
-    def edge_band(b, theta, centre):
-        from_east, from_west = side_in[b, 0], side_in[b, 1]
-        to_west, to_east = side_out[b, 0], side_out[b, 1]
+    def edge_band(got, given, theta, centre):
+        from_east, from_west = got
+        to_west, to_east = given
         low = jnp.where(lane < 64, pltpu.roll(from_west, 64, 1), pltpu.roll(to_east, 64, 1))
         high = jnp.where(lane < 64, to_west, from_east)
         e1 = jnp.where(even, pltpu.roll(centre, 127, 1), pltpu.roll(high, 1, 1))
@@ -500,14 +516,14 @@
         s2 = jnp.where(row >= 2, 0.0, pltpu.roll(corners, 4, 1))
         return edge_coef(3) * n1 + edge_coef(4) * s1 + edge_coef(5) * (s2 - n2)
 
-    def add_sides(k, centre):
+    def add_sides(k, centre, picked):
         def own(q):
             return jnp.where(spot[0:1] < 64, fixed_out[0, channels + q:channels + q + 1, :],
                              pltpu.roll(fixed_out[1, channels + q:channels + q + 1, :], 64, 1))
 
         from_west = own(2) * centre + jnp.where(even, own(1) * pltpu.roll(centre, 127, 1), 0.0)
         from_east = jnp.where(even, 0.0, own(0) * pltpu.roll(centre, 1, 1)) - own(2) * centre
-        for r in range(lat):
+        for r in picked:
             left = pltpu.roll(from_west, (128 - 2 * r) % 128, 1) if r else from_west
             right = pltpu.roll(from_east, (62 - 2 * r) % 128, 1) if 2 * r != 62 else from_east
             basis[k + 1, r + HALO, :, 0:128] += jnp.where(lane < 2, left, 0.0)
@@ -520,30 +536,35 @@
             rows(k, [2 + GROUP * g + j for j in range(GROUP)], theta, None)
         rows(k, (0, 1, lat - 2, lat - 1), theta, None, bare=True)
 
-        @pl.when(b > 0)
+        dots_two(k, 0, lat)
+        more = b + 1 < BLOCKS
+        for part in range(2):
+            lon_copy(b, part, 0).wait()
+            lon_copy(b, part, 1).wait()
+            if part == 0:
+                @pl.when(b == 0)
+                def _():
+                    fix_side(0).wait()
+                    fix_side(1).wait()
+
+            got = both(side_in, b, part)
+            centre = middle(got)
+            add_sides(k, centre, sided[part])
+            band[...] = edge_band(got, both(side_out, b, part), theta, centre)
+            beside = band[...]
+            if part:
+                rows(k + 1, (4, 5, lat - 6, lat - 5), after, beside)
+            else:
+                for g in range((lat - 12) // GROUP):
+                    rows(k + 1, [6 + GROUP * g + j for j in range(GROUP)], after, beside)
+
+        @pl.when(more)
         def _():
-            dots(k - 1, 0, lat)
-
-        dots(k, 0, lat)
-        lon_copy(b, 0).wait()
-        lon_copy(b, 1).wait()
-
-        @pl.when(b == 0)
-        def _():
-            fix_side(0).wait()
-            fix_side(1).wait()
-
-        centre = middle(b)
-        add_sides(k, centre)
-        band[...] = edge_band(b, theta, centre)
-        beside = band[...]
-        for g in range((lat - 8) // GROUP):
-            rows(k + 1, [4 + GROUP * g + j for j in range(GROUP)], after, beside)
+            send_sides(b + 1, 0)
 
         @pl.when(b + 1 == BLOCKS)
         def _():
-            dots(k + 1, 4, lat - 8)
-            dots(k + 2, 4, lat - 8)
+            dots_two(k + 2, 4, lat - 8)
 
         def corners_in(way):
             turn_copy(b, way, 0).wait_recv()
@@ -566,7 +587,6 @@
         basis[k + 1, HALO + lat - 1] += coef[lat + 1, 3:4, :] * north - coef[lat + 1, 5:6, :] * basis[k, HALO + lat + 1]
         basis[k + 1, HALO + lat - 2] -= coef[lat, 5:6, :] * north
         rows(k + 1, (2, 3, lat - 4, lat - 3), after, beside)
-        more = b + 1 < BLOCKS
 
         @pl.when(more)
         def _():
@@ -587,7 +607,7 @@
         def _():
             send_corners(b + 1)
             each_lat(lambda way: lat_copy(b + 1, way, 1).start())
-            send_sides(b + 1)
+            send_sides(b + 1, 1)
 
         for n in range(min(words, BLOCKS)):
             @pl.when(b == n)
@@ -625,7 +645,8 @@
         lat_copy(0, way, 0).start()
 
     each_lat(first_rows)
-    send_sides(0)
+    send_sides(0, 0)
+    send_sides(0, 1)
     for copy in small:
         copy.wait()
 
@@ -668,42 +689,30 @@
         hear_word(n - 1)
         if n < words:
             spread_word(n)
-    dots_rest()
+    dots_two(ITERS, lat - 4, 8, True)
 
     sums = jnp.concatenate(
         [jnp.sum(gram_acc[n], axis=0, keepdims=True) for n in range(len(PAIRS))]
         + [jnp.zeros((128 - len(PAIRS), 128), jnp.float32)], axis=0)
     flat = lax.dot_general(jnp.ones((8, 128), jnp.float32), sums, (((1,), (1,)), ((), ())), precision=HI,
                            preferred_element_type=jnp.float32)
-    mine[...] = flat[0:1, :]
     slots[me] = flat[0:1, :]
 
-    def share(o):
-        other = lax.rem(me + o, total)
-        return pltpu.make_async_remote_copy(
-            src_ref=mine, dst_ref=slots.at[me], send_sem=red_send.at[o], recv_sem=red_recv.at[me],
-            device_id=(other // ny, lax.rem(other, ny)), device_id_type=MESH)
-
-    def take(o):
-        other = lax.rem(me + total - o, total)
-        return pltpu.make_async_remote_copy(
-            src_ref=mine, dst_ref=slots.at[other], send_sem=red_send.at[o], recv_sem=red_recv.at[other],
-            device_id=(other // ny, lax.rem(other, ny)), device_id_type=MESH)
-
-    def give(o, _):
-        share(o).start()
-        return 0
-
-    def get(o, _):
-        take(o).wait_recv()
-        share(o).wait_send()
-        return 0
-
-    lax.fori_loop(1, total, give, 0)
-    lax.fori_loop(1, total, get, 0)
-    whole = slots[0]
-    for n in range(1, total):
-        whole = whole + slots[n]
+    def share(to):
+        return copy_to(slots.at[me], slots.at[me], red_send.at[0], red_recv.at[0], to)
+
+    def wrap(v, n):
+        return jnp.where(v >= n, v - n, v)
+
+    for dx in range(nx):
+        for dy in range(ny):
+            if dx or dy:
+                share((wrap(ix + dx, nx), wrap(iy + dy, ny))).start()
+    others = slots.at[pl.ds(0, total - 1)]
+    everyone = copy_to(others, others, red_send.at[0], red_recv.at[0], (east, iy))
+    everyone.wait_recv()
+    everyone.wait_send()
+    whole = tree([slots[n] for n in range(total)])
     gram = [[None] * (ITERS + 1) for _ in range(ITERS + 1)]
     for n, (k, i) in enumerate(PAIRS):
         gram[k][i] = gram[i][k] = jnp.broadcast_to(whole[:, n:n + 1], (8, 128))
@@ -769,22 +778,21 @@
                 pltpu.VMEM((lat + 4, 8, lon), f32),
                 pltpu.VMEM((GROUP * channels, 3 * GROUP * channels), jnp.bfloat16),
                 pltpu.VMEM((channels, 3 * channels), jnp.bfloat16),
-                pltpu.VMEM((BLOCKS, 2, channels, 128), f32),
-                pltpu.VMEM((BLOCKS, 2, channels, 128), f32),
+                pltpu.VMEM((BLOCKS, 2, 2, channels, 128), f32),
+                pltpu.VMEM((BLOCKS, 2, 2, channels, 128), f32),
                 pltpu.VMEM((channels, 128), f32),
                 pltpu.VMEM((2, channels + 8, 128), f32),
                 pltpu.VMEM((2, channels + 8, 128), f32),
                 pltpu.VMEM((BLOCKS, 4, 2, 128), f32),
                 pltpu.VMEM((BLOCKS, 2, 128), f32),
                 pltpu.VMEM((len(PAIRS), 8, 128), f32),
-                pltpu.VMEM((1, 128), f32),
                 pltpu.VMEM((nx * ny, 1, 128), f32),
                 pltpu.VMEM((channels, channels), f32), pltpu.VMEM((lat, lon), f32), pltpu.VMEM((lat, lon), f32),
                 pltpu.VMEM((2, 2, 2, lon), f32), pltpu.VMEM((2, 8, 128), f32), pltpu.VMEM((2, channels, 128), f32),
                 dma((2, channels)), dma((3,)),
-                dma((BLOCKS, 2, 2)), dma((BLOCKS, 2, 2)), dma((BLOCKS, 2)), dma((BLOCKS, 2)),
+                dma((BLOCKS, 2, 2)), dma((BLOCKS, 2, 2)), dma((BLOCKS, 2, 2)), dma((BLOCKS, 2, 2)),
                 dma((BLOCKS, 4)), dma((BLOCKS, 4)), dma((4, 2)), dma((4, 2)),
-                dma((nx * ny,)), dma((nx * ny,)), pltpu.SemaphoreType.REGULAR((8,)),
+                dma((1,)), dma((1,)), pltpu.SemaphoreType.REGULAR((8,)),
             ],
             compiler_params=pltpu.CompilerParams(
                 collective_id=0, has_side_effects=True, vmem_limit_bytes=24 * 1024 * 1024),

time: 39.2 us -> 37.3 us (0.952)
  Pallas kernels: 38.3 us -> 36.5 us
    pallas_call x1, Pallas kernels: 35.2 us -> 33.4 us  [per_device(): pl.pallas_call(functools.partial(kernel, nx, ny), out_shape=(pltpu.VMEM((...]
where the time goes in v3:
time: 37.3 us; the launch traced here: 37.1 us
  Pallas kernels  36.5 us (98%)
  between operations  0.64 us (2%)
    pallas_call x1, Pallas kernels, per_device(): pl.pallas_call(functools.partial(kernel, nx, ny), out_shape=(pltpu.VMEM((...  33.4 us
    pallas_call x1, Pallas kernels, per_device(): pl.pallas_call(finish, out_shape=(shape, shape), in_specs=[vmem, vmem], o...  3.11 us

profile of v3, /device:TPU:0, one launch (start us, length us, event | category | flops | bytes accessed | tf_op | source)
XLA Modules:
  0.0 37.1 jit_solution(11597805385238999139)
XLA Ops:
  0.6 33.4 %shard_map.68 = (f32[9,40,16,256]{3,2,1,0:T(8,128)S(1)}, f32[17,8,128]{2,1,0:T(8,128)S(1)}) custom-call(f32[16,32,256]{2,1,0:T(8,128)} %f_hbm.1, f32[16,32,256]{2,1,0:T(8,128)} %d_hbm.1, f32[16,16]{1,0:T(8,128)} %c_hbm.1, f32[32,256]{1,0:T(8,128)} %wl_hbm.1, f32[32,256]{1,0:T(8,128)} %wa_hbm.1), custom_call_target="tpu_custom_call" | custom-call | tf_op jit(solution)/shard_map/pallas_call | solution.py:771
  34.0 3.1 %shard_map.69 = (f32[16,32,256]{2,1,0:T(8,128)}, f32[16,32,256]{2,1,0:T(8,128)}) custom-call(f32[9,40,16,256]{3,2,1,0:T(8,128)S(1)} %get-tuple-element.4.b_ref, f32[17,8,128]{2,1,0:T(8,128)S(1)} %get-tuple-element.5.w_ref), custom_call_target="tpu_custom_call" | custom-call | tf_op jit(solution)/shard_map/pallas_call | solution.py:801

commit v4 on v3

--- a/solution.py
+++ b/solution.py
@@ -133,12 +133,13 @@
     return far_lat, far_lon
 
 
-def kernel(nx, ny, f_hbm, d_hbm, c_hbm, wl_hbm, wa_hbm, basis, splats,
+def kernel(nx, ny, f_hbm, d_hbm, c_hbm, wl_hbm, wa_hbm, padded, splats,
            diag, coef, block, single, side_in, side_out, band, fixed_in, fixed_out, corner_in, corner_out,
            gram_acc, slots, c_ref, wl_ref, wa_ref, wind_in, kx_in, turned,
            in_sem, wind_sem, lat_send, lat_recv, lon_send, lon_recv, turn_send, turn_recv, fix_send, fix_recv, red_send, red_recv, word):
     channels, lat, lon = f_hbm.shape
     tiles = lon // 128
+    basis = padded.at[:, :, pl.ds(0, channels), :]
     total = nx * ny
     ix, iy = lax.axis_index("gx"), lax.axis_index("gy")
     me = ix * ny + iy
@@ -576,11 +577,8 @@
                     copy.wait_recv()
                 fill_coef(wind_in[0, way], wind_in[1, way], kx_in[way, 6:8] if way else kx_in[way, 0:2], 0 if way else lat + 2)
 
-        arrive_lat(corners_in)
-        turned[0] = take_corners(b)
-        turned[1] = band[...] + edge_turn(turned[0])
         arrive_lat(lambda way: lat_copy(b, way, 1).wait_recv())
-        beside = turned[1]
+        beside = band[...]
         south, north = basis[k, HALO - 1], basis[k, HALO + lat]
         basis[k + 1, HALO] += coef[2, 4:5, :] * south + coef[2, 5:6, :] * basis[k, HALO - 2]
         basis[k + 1, HALO + 1] += coef[3, 5:6, :] * south
@@ -591,6 +589,10 @@
         @pl.when(more)
         def _():
             each_lat(lambda way: lat_copy(b + 1, way, 0).start())
+
+        arrive_lat(corners_in)
+        turned[0] = take_corners(b)
+        turned[1] = band[...] + edge_turn(turned[0])
 
         def far_in(way):
             lat_copy(b, way, 0).wait_recv()
@@ -770,7 +772,7 @@
 
         basis, weights = pl.pallas_call(
             functools.partial(kernel, nx, ny),
-            out_shape=(pltpu.VMEM((ITERS + 1, lat + 2 * HALO, channels, lon), f32), pltpu.VMEM((2 * ITERS + 1, 8, 128), f32)),
+            out_shape=(pltpu.VMEM((ITERS + 1, lat + 2 * HALO + 1, channels + 8, lon), f32), pltpu.VMEM((2 * ITERS + 1, 8, 128), f32)),
             in_specs=[hbm] * 5,
             out_specs=(vmem, vmem),
             scratch_shapes=[

time: 37.3 us -> 36.8 us (0.987)
  Pallas kernels: 36.5 us -> 35.9 us
    pallas_call x1, Pallas kernels: 33.4 us -> 32.8 us  [per_device(): pl.pallas_call(functools.partial(kernel, nx, ny), out_shape=(pltpu.VMEM((...]
where the time goes in v4:
time: 36.8 us; the launch traced here: 36.5 us
  Pallas kernels  35.9 us (98%)
  between operations  0.64 us (2%)
    pallas_call x1, Pallas kernels, per_device(): pl.pallas_call(functools.partial(kernel, nx, ny), out_shape=(pltpu.VMEM((...  32.8 us
    pallas_call x1, Pallas kernels, per_device(): pl.pallas_call(finish, out_shape=(shape, shape), in_specs=[vmem, vmem], o...  3.12 us

profile of v4, /device:TPU:0, one launch (start us, length us, event | category | flops | bytes accessed | tf_op | source)
XLA Modules:
  0.0 36.5 jit_solution(4401798634417202613)
XLA Ops:
  0.6 32.8 %shard_map.68 = (f32[9,41,24,256]{3,2,1,0:T(8,128)S(1)}, f32[17,8,128]{2,1,0:T(8,128)S(1)}) custom-call(f32[16,32,256]{2,1,0:T(8,128)} %f_hbm.1, f32[16,32,256]{2,1,0:T(8,128)} %d_hbm.1, f32[16,16]{1,0:T(8,128)} %c_hbm.1, f32[32,256]{1,0:T(8,128)} %wl_hbm.1, f32[32,256]{1,0:T(8,128)} %wa_hbm.1), custom_call_target="tpu_custom_call" | custom-call | tf_op jit(solution)/shard_map/pallas_call | solution.py:773
  33.4 3.1 %shard_map.69 = (f32[16,32,256]{2,1,0:T(8,128)}, f32[16,32,256]{2,1,0:T(8,128)}) custom-call(f32[9,41,24,256]{3,2,1,0:T(8,128)S(1)} %get-tuple-element.4.b_ref, f32[17,8,128]{2,1,0:T(8,128)S(1)} %get-tuple-element.5.w_ref), custom_call_target="tpu_custom_call" | custom-call | tf_op jit(solution)/shard_map/pallas_call | solution.py:803

commit v5 on v4

--- a/solution.py
+++ b/solution.py
@@ -640,13 +640,12 @@
     for copy in loads[0]:
         copy.wait()
     pl.semaphore_wait(barrier, 2 + jnp.where(iy > 0, 3, 0) + jnp.where(iy < ny - 1, 3, 0))
-    send_corners(0)
-
     def first_rows(way):
         lat_copy(0, way, 1).start()
         lat_copy(0, way, 0).start()
 
     each_lat(first_rows)
+    send_corners(0)
     send_sides(0, 0)
     send_sides(0, 1)
     for copy in small:

time: 36.8 us -> 36.6 us (level)
  no operation moved by 1% of the time
where the time goes in v5:
time: 36.6 us; the launch traced here: 36.4 us
  Pallas kernels  35.8 us (98%)
  between operations  0.64 us (2%)
    pallas_call x1, Pallas kernels, per_device(): pl.pallas_call(functools.partial(kernel, nx, ny), out_shape=(pltpu.VMEM((...  32.6 us
    pallas_call x1, Pallas kernels, per_device(): pl.pallas_call(finish, out_shape=(shape, shape), in_specs=[vmem, vmem], o...  3.12 us

profile of v5, /device:TPU:0, one launch (start us, length us, event | category | flops | bytes accessed | tf_op | source)
XLA Modules:
  0.0 36.4 jit_solution(13586528786360091584)
XLA Ops:
  0.6 32.6 %shard_map.68 = (f32[9,41,24,256]{3,2,1,0:T(8,128)S(1)}, f32[17,8,128]{2,1,0:T(8,128)S(1)}) custom-call(f32[16,32,256]{2,1,0:T(8,128)} %f_hbm.1, f32[16,32,256]{2,1,0:T(8,128)} %d_hbm.1, f32[16,16]{1,0:T(8,128)} %c_hbm.1, f32[32,256]{1,0:T(8,128)} %wl_hbm.1, f32[32,256]{1,0:T(8,128)} %wa_hbm.1), custom_call_target="tpu_custom_call" | custom-call | tf_op jit(solution)/shard_map/pallas_call | solution.py:772
  33.3 3.1 %shard_map.69 = (f32[16,32,256]{2,1,0:T(8,128)}, f32[16,32,256]{2,1,0:T(8,128)}) custom-call(f32[9,41,24,256]{3,2,1,0:T(8,128)S(1)} %get-tuple-element.4.b_ref, f32[17,8,128]{2,1,0:T(8,128)S(1)} %get-tuple-element.5.w_ref), custom_call_target="tpu_custom_call" | custom-call | tf_op jit(solution)/shard_map/pallas_call | solution.py:802

commit v6 on v5

--- a/solution.py
+++ b/solution.py
@@ -50,16 +50,15 @@
         moved = apply_to(coords[j])
         column = []
         for i in range(j + 1):
-            column.append(functools.reduce(lambda a, b: a + b, [images[i][k] * moved[k] for k in range(j + 2)]))
+            column.append(tree([images[i][k] * moved[k] for k in range(j + 2)]))
         left = list(moved)
-        for i in range(j + 1):
-            for k in range(i + 1):
-                left[k] = left[k] - column[i] * coords[i][k]
+        for k in range(j + 1):
+            left[k] = left[k] - tree([column[i] * coords[i][k] for i in range(k, j + 1)])
         image = [
-            functools.reduce(lambda a, b: a + b, [gram[r][k] * left[k] for k in range(j + 2)])
+            tree([gram[r][k] * left[k] for k in range(j + 2)])
             for r in range(ITERS + 1)
         ]
-        norm_sq = functools.reduce(lambda a, b: a + b, [image[k] * left[k] for k in range(j + 2)])
+        norm_sq = tree([image[k] * left[k] for k in range(j + 2)])
         subdiag = jnp.sqrt(jnp.maximum(norm_sq, 0.0) + GUARD)
         column.append(subdiag)
         heights.append(column)
@@ -607,8 +606,8 @@
 
         @pl.when(more)
         def _():
+            each_lat(lambda way: lat_copy(b + 1, way, 1).start())
             send_corners(b + 1)
-            each_lat(lambda way: lat_copy(b + 1, way, 1).start())
             send_sides(b + 1, 1)
 
         for n in range(min(words, BLOCKS)):

time: 36.6 us -> 36.6 us (level)
  no operation moved by 1% of the time
where the time goes in v6:
time: 36.6 us; the launch traced here: 36.4 us
  Pallas kernels  35.8 us (98%)
  between operations  0.64 us (2%)
    pallas_call x1, Pallas kernels, per_device(): pl.pallas_call(functools.partial(kernel, nx, ny), out_shape=(pltpu.VMEM((...  32.7 us
    pallas_call x1, Pallas kernels, per_device(): pl.pallas_call(finish, out_shape=(shape, shape), in_specs=[vmem, vmem], o...  3.12 us

profile of v6, /device:TPU:0, one launch (start us, length us, event | category | flops | bytes accessed | tf_op | source)
XLA Modules:
  0.0 36.4 jit_solution(6016636644466771088)
XLA Ops:
  0.6 32.7 %shard_map.68 = (f32[9,41,24,256]{3,2,1,0:T(8,128)S(1)}, f32[17,8,128]{2,1,0:T(8,128)S(1)}) custom-call(f32[16,32,256]{2,1,0:T(8,128)} %f_hbm.1, f32[16,32,256]{2,1,0:T(8,128)} %d_hbm.1, f32[16,16]{1,0:T(8,128)} %c_hbm.1, f32[32,256]{1,0:T(8,128)} %wl_hbm.1, f32[32,256]{1,0:T(8,128)} %wa_hbm.1), custom_call_target="tpu_custom_call" | custom-call | tf_op jit(solution)/shard_map/pallas_call | solution.py:771
  33.3 3.1 %shard_map.69 = (f32[16,32,256]{2,1,0:T(8,128)}, f32[16,32,256]{2,1,0:T(8,128)}) custom-call(f32[9,41,24,256]{3,2,1,0:T(8,128)S(1)} %get-tuple-element.4.b_ref, f32[17,8,128]{2,1,0:T(8,128)S(1)} %get-tuple-element.5.w_ref), custom_call_target="tpu_custom_call" | custom-call | tf_op jit(solution)/shard_map/pallas_call | solution.py:801
